TPU v7x, 32 devices: a whole 2x2x4 slice. The times are simulated.
32 devices in a mesh: gx: 4 (over y, x), gy: 2 (over core), gz: 4 (over z).
Axes of the slice: x: 2, y: 2, z: 4, core: 2. Of those that a mesh axis runs over, the one named last changes fastest.
Arguments:
- pair_blocks: float32 [529, 1024], P(None, ('gx', 'gy', 'gz')), may hold values from -6 to 6
- basis_map: float32 [529, 64], replicated, may hold values from -0.25 to 0.25
- pair_cells: int32 [3, 1024], P(None, ('gx', 'gy', 'gz')), may hold values from 0 to 511, as said below
- pair_offsets: float32 [3, 1024], P(None, ('gx', 'gy', 'gz')), may hold values from 0 to 1
- exponent_index: int32 [1024], P(('gx', 'gy', 'gz')), may hold values from 0 to 15
- radius_index: int32 [1024], P(('gx', 'gy', 'gz')), may hold values from 0 to 4
- exponents: float32 [16], replicated, may hold values from 7 to 9
Outputs:
- density: float32 [32, 64, 512], P('gx', 'gy', 'gz')
- spectrum: float32 [2, 512, 64, 32], P(None, ('gy', 'gz'), 'gx')
Inputs may be any that keep to these rules, and one draw needn't show every extreme that they name: The y of pair_cells column p lies among the 32 cells, and its z among the 128 cells, of the gy and gz index of the device that holds column p. Of the pairs that one device holds at most 16 have x in the same run of 8 cells that one gx index holds, and in every draw some such run gets exactly 16 from every device.
All inputs are finite; a program needn't handle non-finite values.
Results may differ from a plain program's by a relative error of at most 0.0003.
Values sent between devices are 32-bit elements; how exact they have to be, the bound alone decides.
A program may use at most 64 MiB of HBM per device.

v0:
```python
import functools
import math

import jax
import jax.numpy as jnp
import numpy as np
from jax import lax
from jax.experimental import pallas as pl
from jax.experimental.pallas import tpu as pltpu
from jax.sharding import PartitionSpec as P

DEG = 3
HALO = 8
CX = 8
CY = 32
CZ = 128
SIDE = DEG + 1
LANES = 128
SPAN = 32
VMEM_LIMIT = 40 << 20
GROUP = 24

highest = lax.Precision.HIGHEST
f32 = jnp.float32
bf16 = jnp.bfloat16


def iota_f(shape, dim):
    return lax.broadcasted_iota(jnp.int32, shape, dim).astype(f32)


def cos_sin(turns):
    r = turns - jnp.floor(turns + 0.5)
    t = r * math.pi
    t2 = t * t
    s = t * _poly(t2, [(-1) ** n / math.factorial(2 * n + 1) for n in range(7)])
    c = _poly(t2, [(-1) ** n / math.factorial(2 * n) for n in range(8)])
    return 1.0 - 2.0 * s * s, 2.0 * s * c


def _poly(x, coefs):
    out = jnp.full_like(x, coefs[-1])
    for a in reversed(coefs[:-1]):
        out = out * x + a
    return out


def wrapped(cells, centre, total):
    d = cells - centre
    d = jnp.where(d < -HALO, d + total, d)
    return jnp.where(d > total - 1 - HALO, d - total, d)


def factors(offset, within, rate, radius):
    u = offset - within
    env = jnp.exp(-rate * u * u) * (jnp.abs(offset) <= radius).astype(f32)
    s = u * (1.0 / HALO)
    out = [env]
    for _ in range(DEG):
        out.append(out[-1] * s)
    return out


def split(v):
    hi = v.astype(bf16)
    return hi, (v - hi.astype(f32)).astype(bf16)


def nt(a, b):
    return lax.dot_general(a, b, (((1,), (1,)), ((), ())), preferred_element_type=f32)


def spectral(frequency, length, centre, within, rate, radius, table):
    n = frequency.shape[0]
    offs = iota_f((SPAN, LANES), 0) - HALO
    four = jnp.concatenate(factors(offs, within, rate, radius), axis=1)
    hi, lo = split(four)
    part = jnp.dot(
        table, jnp.concatenate([hi, lo, hi], axis=0), preferred_element_type=f32
    )
    pc, ps = cos_sin(frequency * centre * (1.0 / length))
    out = []
    for d in range(SIDE):
        a = part[:n, d * LANES : (d + 1) * LANES]
        b = part[n:, d * LANES : (d + 1) * LANES]
        out.append((a * pc + b * ps, b * pc - a * ps))
    return out


def span_table(frequency, length):
    offs = iota_f((1, SPAN), 1) - HALO
    c, s = cos_sin(frequency * offs * (1.0 / length))
    hi, lo = split(jnp.concatenate([c, -s], axis=0))
    return jnp.concatenate([hi, hi, lo], axis=1)


def chunk_work(prm, sizes, place, refs):
    nx, ny, nz, nky, nkz = sizes
    gx, gy, gz, kz0 = place
    (h_s, hd_s, fxl_s, t_hi, t_lo, d_hi, d_lo, z_s, zd_s, ytab, ztab, acc, dacc) = refs
    rows = lambda a: prm[a : a + 1, :]
    base = SIDE**3
    cx, cy, cz, ox, oy, oz, rate, radius = [rows(base + n) for n in range(8)]
    kyc = iota_f((nky, 1), 0) + (gx * nky).astype(f32)
    kzc = iota_f((nkz, 1), 0) + (kz0 * nkz).astype(f32)
    fy = spectral(kyc, ny, cy, oy, rate, radius, ytab[...])
    fz = spectral(kzc, nz, cz, oz, rate, radius, ztab[...])
    fx = factors(wrapped(iota_f((nx, LANES), 0), cx, float(nx)), ox, rate, radius)
    fyl = factors(
        wrapped(iota_f((CY, LANES), 0) + (gy * CY).astype(f32), cy, float(ny)), oy, rate, radius
    )
    fzl = factors(
        wrapped(iota_f((CZ, LANES), 0) + (gz * CZ).astype(f32), cz, float(nz)), oz, rate, radius
    )
    fxl = factors(
        wrapped(iota_f((CX, LANES), 0) + (gx * CX).astype(f32), cx, float(nx)), ox, rate, radius
    )
    for i in range(SIDE):
        fxl_s[i] = fxl[i]
    for k in range(SIDE):
        lanes = slice(k * LANES, (k + 1) * LANES)
        zhi, zlo = split(jnp.concatenate(fz[k], axis=0))
        z_s[: 2 * nkz, lanes] = zhi
        z_s[2 * nkz :, lanes] = zlo
        zhi, zlo = split(fzl[k])
        zd_s[:CZ, lanes] = zhi
        zd_s[CZ:, lanes] = zlo
        for i in range(SIDE):
            re = im = de = None
            for j in range(SIDE):
                c = rows((i * SIDE + j) * SIDE + k)
                re = c * fy[j][0] if re is None else re + c * fy[j][0]
                im = c * fy[j][1] if im is None else im + c * fy[j][1]
                de = c * fyl[j] if de is None else de + c * fyl[j]
            h_s[k * SIDE + i, :nky] = re
            h_s[k * SIDE + i, nky:] = im
            hd_s[k * SIDE + i] = de
    def build(r):
        for k in range(SIDE):
            v = None
            for i in range(SIDE):
                w = h_s[k * SIDE + i, r : r + 1, :] * fx[i]
                v = w if v is None else v + w
            hi, lo = split(v)
            t_hi[r * nx : (r + 1) * nx, k * LANES : (k + 1) * LANES] = hi
            t_lo[r * nx : (r + 1) * nx, k * LANES : (k + 1) * LANES] = lo

    def build_cell(x):
        for k in range(SIDE):
            v = None
            for i in range(SIDE):
                w = hd_s[k * SIDE + i] * fxl_s[i, x : x + 1, :]
                v = w if v is None else v + w
            hi, lo = split(v)
            d_hi[x * CY : (x + 1) * CY, k * LANES : (k + 1) * LANES] = hi
            d_lo[x * CY : (x + 1) * CY, k * LANES : (k + 1) * LANES] = lo

    def add(target, hi, lo, z, s, n):
        if n % LANES == 0:
            both = nt(hi[s], z[...])
            more = both[:, :n] + both[:, n:]
        else:
            more = nt(hi[s], z[:n]) + nt(hi[s], z[n:])
        target[s] = target[s] + (more + nt(lo[s], z[:n]))

    block = 256
    per = max(block // nx, 1)
    block = per * nx
    for x in range(CX):
        build_cell(x)
    late = [lambda: add(dacc, d_hi, d_lo, zd_s, slice(0, CX * CY), CZ)]
    for b in range(2 * nky // per):
        for r in range(b * per, (b + 1) * per):
            build(r)
        late.pop()()
        late.append(
            lambda b=b: add(acc, t_hi, t_lo, z_s, slice(b * block, (b + 1) * block), 2 * nkz)
        )
    late.pop()()


def finish(sizes, acc, dacc, xtab, dens_ref, spec_ref):
    nx, ny, nz, nky, nkz = sizes
    dens_ref[...] = dacc[...]
    wide = max(nx, LANES)
    per = wide // nx
    for g in range(nky // per):
        re = acc[g * wide : (g + 1) * wide]
        im = acc[nky * nx + g * wide : nky * nx + (g + 1) * wide]
        both = jnp.concatenate([re[:, :nkz] - im[:, nkz:], re[:, nkz:] + im[:, :nkz]], axis=1)
        q = jnp.dot(xtab[...], both, precision=highest, preferred_element_type=f32)
        s = slice(g * wide, (g + 1) * wide)
        spec_ref[0, s] = q[:wide, :nkz] + q[wide:, nkz:]
        spec_ref[1, s] = q[:wide, nkz:] - q[wide:, :nkz]


def scratches(sizes):
    nx, ny, nz, nky, nkz = sizes
    m = 2 * nky * nx
    k = SIDE * LANES
    return [
        pltpu.VMEM((SIDE * SIDE, 2 * nky, LANES), f32),
        pltpu.VMEM((SIDE * SIDE, CY, LANES), f32),
        pltpu.VMEM((SIDE, CX, LANES), f32),
        pltpu.VMEM((m, k), bf16),
        pltpu.VMEM((m, k), bf16),
        pltpu.VMEM((CX * CY, k), bf16),
        pltpu.VMEM((CX * CY, k), bf16),
        pltpu.VMEM((4 * nkz, k), bf16),
        pltpu.VMEM((2 * CZ, k), bf16),
        pltpu.VMEM((2 * nky, 3 * SPAN), bf16),
        pltpu.VMEM((2 * nkz, 3 * SPAN), bf16),
    ]


def start_work(sizes, place, refs):
    nx, ny, nz, nky, nkz = sizes
    gx, gy, gz, kz0 = place
    ytab, ztab, acc, dacc = refs[-4:]
    kyc = iota_f((nky, 1), 0) + (gx * nky).astype(f32)
    kzc = iota_f((nkz, 1), 0) + (kz0 * nkz).astype(f32)
    ytab[...] = span_table(kyc, ny)
    ztab[...] = span_table(kzc, nz)
    for r in (acc, dacc):
        r[...] = jnp.zeros_like(r)


def where_am_i():
    gx, gy, gz = (lax.axis_index(a) for a in ("gx", "gy", "gz"))
    return gx, gy, gz, gy * lax.axis_size("gz") + gz


def unpack(blocks, prm):
    owner = lax.broadcasted_iota(jnp.int32, (GROUP, LANES), 1) // (LANES // len(blocks))
    for g in range(prm.shape[0] // GROUP):
        v = None
        for d, block in enumerate(blocks):
            shift = (d - g) % len(blocks) * (LANES // len(blocks))
            w = pltpu.roll(block, shift, 1) if shift else block
            v = w if v is None else jnp.where(owner == d, w, v)
        prm[g * GROUP : (g + 1) * GROUP] = v


def kernel(sizes, counts, own_ref, acc, dacc, prm, cols, *refs):
    refs, (send_z, recv_z, send_c, recv_c) = (*refs[:-4], acc, dacc), refs[-4:]
    n_gx, n_gy, n_gz = counts
    place = where_am_i()
    gx, gy, gz = place[:3]
    n_col = n_gx * n_gy

    def along_z(r):
        return gx, gy, lax.rem(gz + n_gz - r, n_gz)

    def along_x(dx):
        return lax.rem(gx + n_gx - dx, n_gx), gy, gz

    def along_y(dy):
        return gx, lax.rem(gy + n_gy - dy, n_gy), gz

    mesh_type = pl.DeviceIdType.MESH
    barrier = pltpu.get_barrier_semaphore()
    for r in range(1, n_gz):
        pl.semaphore_signal(barrier, inc=1, device_id=along_z(r), device_id_type=mesh_type)

    def greet(dx, carry):
        pl.semaphore_signal(barrier, inc=1, device_id=along_x(dx), device_id_type=mesh_type)
        return carry

    lax.fori_loop(1, n_gx, greet, 0)
    for dy in range(1, n_gy):
        pl.semaphore_signal(barrier, inc=1, device_id=along_y(dy), device_id_type=mesh_type)
    cols[0, 0] = own_ref[...]
    start_work(sizes, place, refs)
    pl.semaphore_wait(barrier, n_gz + n_gx + n_gy - 3)

    def copy_z(r):
        return pltpu.make_async_remote_copy(
            src_ref=own_ref,
            dst_ref=cols.at[0, r],
            send_sem=send_z.at[r],
            recv_sem=recv_z.at[r],
            device_id=along_z(r),
            device_id_type=mesh_type,
        )

    def copy_c(source, c, target):
        return pltpu.make_async_remote_copy(
            src_ref=cols.at[source],
            dst_ref=cols.at[c],
            send_sem=send_c.at[c],
            recv_sem=recv_c.at[c],
            device_id=target,
            device_id_type=mesh_type,
        )

    for r in range(1, n_gz):
        copy_z(r).start()
    for r in range(1, n_gz):
        copy_z(r).wait_recv()

    def send(dx, carry):
        copy_c(0, dx * n_gy, along_x(dx)).start()
        return carry

    lax.fori_loop(1, n_gx, send, 0)

    def step(c, carry):
        @pl.when(c > 0)
        def _():
            copy_c(0, c, along_x(1)).wait_recv()

        @pl.when(c % n_gy == 0)
        def _():
            for dy in range(1, n_gy):
                copy_c(c, c + dy, along_y(dy)).start()

        unpack([cols[c, r] for r in range(n_gz)], prm)
        chunk_work(prm, sizes, place, refs)
        return carry

    lax.fori_loop(0, n_col, step, 0)
    for r in range(1, n_gz):
        copy_z(r).wait_send()

    def drain(c, carry):
        copy_c(0, c, along_x(1)).wait_send()
        return carry

    lax.fori_loop(1, n_col, drain, 0)


def x_table(nx, total):
    wide = max(nx, LANES)
    idx = np.arange(nx)
    angle = (idx[:, None] * idx[None, :] % nx) * (2.0 * math.pi / nx)
    eye = np.eye(wide // nx)
    scale = 1.0 / math.sqrt(total)
    return np.concatenate(
        [np.kron(eye, np.cos(angle)), np.kron(eye, np.sin(angle))], axis=0
    ).astype(np.float32) * np.float32(scale)


def shards(
    pair_blocks, basis_map, pair_cells, pair_offsets, exponent_index, radius_index, exponents
):
    n_gx, n_gy, n_gz = (lax.axis_size(a) for a in ("gx", "gy", "gz"))
    nx, ny, nz = CX * n_gx, CY * n_gy, CZ * n_gz
    sizes = (nx, ny, nz, ny // n_gx, nz // (n_gy * n_gz))
    nky, nkz = sizes[3:]
    selector = (
        exponent_index[None, :] == jnp.arange(exponents.shape[0], dtype=jnp.int32)[:, None]
    ).astype(f32)
    radius = (HALO - radius_index).astype(f32)
    rate = jnp.sum(exponents[:, None] * selector, axis=0) / (radius * radius)
    coefs = jnp.dot(basis_map.T, pair_blocks, precision=highest)
    prm = jnp.concatenate(
        [coefs, pair_cells.astype(f32), pair_offsets, rate[None], radius[None]], axis=0
    )
    pair_dev = prm.shape[1]
    assert prm.shape[0] == 3 * GROUP and n_gz * pair_dev == LANES and n_gz >= 3
    groups = [prm[g * GROUP : (g + 1) * GROUP] for g in range(3)]
    groups.append(jnp.zeros((GROUP, LANES - 3 * pair_dev), f32))
    own = jnp.concatenate(groups, axis=1)
    n_col = n_gx * n_gy
    in_vmem = pl.BlockSpec(memory_space=pltpu.VMEM)
    acc, dacc = pl.pallas_call(
        functools.partial(kernel, sizes, (n_gx, n_gy, n_gz)),
        out_shape=[
            jax.ShapeDtypeStruct((2 * nky * nx, 2 * nkz), f32),
            jax.ShapeDtypeStruct((CX * CY, CZ), f32),
        ],
        in_specs=[in_vmem],
        out_specs=[in_vmem] * 2,
        scratch_shapes=[
            pltpu.VMEM((3 * GROUP, LANES), f32),
            pltpu.VMEM((n_col, n_gz, GROUP, LANES), f32),
            *scratches(sizes),
            pltpu.SemaphoreType.DMA((n_gz,)),
            pltpu.SemaphoreType.DMA((n_gz,)),
            pltpu.SemaphoreType.DMA((n_col,)),
            pltpu.SemaphoreType.DMA((n_col,)),
        ],
        compiler_params=pltpu.CompilerParams(
            collective_id=0, has_side_effects=True, vmem_limit_bytes=VMEM_LIMIT
        ),
    )(own)
    dens, spec = pl.pallas_call(
        functools.partial(finish, sizes),
        out_shape=[
            jax.ShapeDtypeStruct((CX * CY, CZ), f32),
            jax.ShapeDtypeStruct((2, nky * nx, nkz), f32),
        ],
        in_specs=[in_vmem] * 3,
        out_specs=[in_vmem] * 2,
        compiler_params=pltpu.CompilerParams(vmem_limit_bytes=VMEM_LIMIT),
    )(acc, dacc, jnp.asarray(x_table(nx, nx * ny * nz)))
    return dens.reshape(CX, CY, CZ), spec.reshape(2, nky, nx, nkz).transpose(0, 3, 1, 2)


def solution(mesh):
    placed = (
        P(None, ("gx", "gy", "gz")),
        P(),
        P(None, ("gx", "gy", "gz")),
        P(None, ("gx", "gy", "gz")),
        P(("gx", "gy", "gz")),
        P(("gx", "gy", "gz")),
        P(),
    )
    return jax.shard_map(
        shards,
        mesh=mesh,
        in_specs=placed,
        out_specs=(P("gx", "gy", "gz"), P(None, ("gy", "gz"), "gx", None)),
        check_vma=False,
    )
```

profile of v0, /device:TPU:0, one launch (start us, length us, event | category | flops | bytes accessed | tf_op | source)
XLA Modules:
  0.0 32.5 jit_solution(18014622138457200800)
XLA Ops:
  0.6 0.0 copy-start
  0.6 0.0 copy-start.4
  0.7 0.8 %select_reduce_fusion = f32[32]{0:T(128)S(1)} fusion(f32[16]{0:T(128)} %param.14, s32[32]{0:T(128)} %param.12), kind=kLoop, calls=%fused_computation.1 | loop fusion | flops 1504 | bytes 320 | tf_op jit(solution)/shard_map/reduce_sum | solution.py:354
  1.5 0.0 copy-done.4
  1.5 0.0 copy-start.3
  1.5 0.1 pad.3.clone
  1.6 0.6 %copy-done.3 = s32[3,32]{1,0:T(4,128)S(1)} copy-done((s32[3,32]{1,0:T(4,128)S(1)}, s32[3,32]{1,0:T(4,128)}, u32[]{:S(2)}) %copy-start.3) | copy-done | bytes 408
  2.2 0.0 copy-done
  2.2 0.0 copy-start.2
  2.2 1.2 %fusion.2 = f32[64,32]{1,0:T(8,128)S(1)} fusion(f32[529,64]{0,1:T(8,128)S(1)} %copy-done, f32[529,32]{0,1:T(8,128)} %param.8), kind=kOutput, calls=%fused_computation.7 | convolution fusion | flops 13000704 | bytes 211328 | tf_op jit(solution)/shard_map/dot_general | solution.py:355
  3.4 0.0 copy-start.1
  3.4 0.0 copy-done.2
  3.4 0.1 maximum_maximum_fusion.own_ref
  3.5 27.4 %shard_map.95 = (f32[1024,128]{1,0:T(8,128)S(1)}, f32[256,128]{1,0:T(8,128)S(1)}) custom-call(f32[24,128]{1,0:T(8,128)S(1)} %maximum_maximum_fusion.own_ref), custom_call_target="tpu_custom_call" | custom-call | tf_op jit(solution)/shard_map/pallas_call | solution.py:366
  30.9 0.0 copy-done.1
  30.9 1.6 %shard_map.96 = (f32[256,128]{1,0:T(8,128)}, f32[2,512,64]{2,1,0:T(8,128)}) custom-call(f32[1024,128]{1,0:T(8,128)S(1)} %get-tuple-element.6.acc, f32[256,128]{1,0:T(8,128)S(1)} %get-tuple-element.7.dacc, f32[256,128]{1,0:T(8,128)S(1)} %copy-done.1), custom_call_target="tpu_custom_call" | custom-call | tf_op jit(solution)/shard_map/pallas_call | solution.py:387
  (7 shorter events, 0.1 us)
Async XLA Ops:
  0.6 1.5 %copy-start = (f32[529,64]{0,1:T(8,128)S(1)}, f32[529,64]{0,1:T(8,128)}, u32[]{:S(2)}) copy-start(f32[529,64]{0,1:T(8,128)} %param.9) | copy-start | bytes 406276
  0.6 0.8 %copy-start.4 = (s32[32]{0:T(128)S(1)}, s32[32]{0:T(128)}, u32[]{:S(2)}) copy-start(s32[32]{0:T(128)} %param.13) | copy-start | bytes 388
  1.5 0.7 %copy-start.3 = (s32[3,32]{1,0:T(4,128)S(1)}, s32[3,32]{1,0:T(4,128)}, u32[]{:S(2)}) copy-start(s32[3,32]{1,0:T(4,128)} %param.10) | copy-start | bytes 1156
  2.2 1.2 %copy-start.2 = (f32[3,32]{1,0:T(4,128)S(1)}, f32[3,32]{1,0:T(4,128)}, u32[]{:S(2)}) copy-start(f32[3,32]{1,0:T(4,128)} %param.11) | copy-start | bytes 1156
  3.4 27.5 %copy-start.1 = (f32[256,128]{1,0:T(8,128)S(1)}, f32[256,128]{1,0:T(8,128)}, u32[]{:S(2)}) copy-start(f32[256,128]{1,0:T(8,128)} %constant.8.clone.xtab) | copy-start | bytes 393220
where the time goes:
time: 32.7 us; the launch traced here: 32.5 us
  Pallas kernels  29 us (89%)
  matrix products  1.17 us (4%)
  other arithmetic  0.89 us (3%)
  local copies, waits for them, and re-layouts  0.73 us (2%)
  between operations  0.73 us (2%)
    pallas_call x1, Pallas kernels, shards(): pl.pallas_call(functools.partial(kernel, sizes, (n_gx, n_gy, n_gz)), out_...  27.4 us
    pallas_call x1, Pallas kernels, shards(): pl.pallas_call(functools.partial(finish, sizes), out_shape=[jax.ShapeDtyp...  1.6 us
    dot_general x1, matrix products, shards(): coefs = jnp.dot(basis_map.T, pair_blocks, precision=highest)  1.17 us
    reduce_sum x1, other arithmetic, shards(): rate = jnp.sum(exponents[:, None] * selector, axis=0) / (radius * radius)  0.8 us

commit v1 on v0

v1 whole, which is shorter than its diff:
```python
import functools
import math

import jax
import jax.numpy as jnp
import ml_dtypes
import numpy as np
from jax import lax
from jax.experimental import pallas as pl
from jax.experimental.pallas import tpu as pltpu
from jax.sharding import PartitionSpec as P

DEG = 3
HALO = 8
CX = 8
CY = 32
CZ = 128
SIDE = DEG + 1
LANES = 128
SPAN = 32
VMEM_LIMIT = 40 << 20
COEFS = SIDE**3
FOLD = 4
TOP = COEFS // FOLD
BLOCK_ROWS = TOP + 8
CYW = CY + 2 * HALO
DEPTH = SIDE * LANES

f32 = jnp.float32
bf16 = jnp.bfloat16


def iota_f(shape, dim):
    return lax.broadcasted_iota(jnp.int32, shape, dim).astype(f32)


def cos_sin(turns):
    r = turns - jnp.floor(turns + 0.5)
    t = r * math.pi
    t2 = t * t
    s = t * _poly(t2, [(-1) ** n / math.factorial(2 * n + 1) for n in range(7)])
    c = _poly(t2, [(-1) ** n / math.factorial(2 * n) for n in range(8)])
    return 1.0 - 2.0 * s * s, 2.0 * s * c


def _poly(x, coefs):
    out = jnp.full_like(x, coefs[-1])
    for a in reversed(coefs[:-1]):
        out = out * x + a
    return out


def wrapped(cells, centre, total):
    d = cells - centre
    d = jnp.where(d < -HALO, d + total, d)
    return jnp.where(d > total - 1 - HALO, d - total, d)


def factors(offset, within, rate, radius):
    u = offset - within
    env = jnp.where(jnp.abs(offset) <= radius, jnp.exp(-rate * u * u), 0.0)
    s = u * (1.0 / HALO)
    out = [env]
    for _ in range(DEG):
        out.append(out[-1] * s)
    return out


def split(v):
    hi = v.astype(bf16)
    return hi, (v - hi.astype(f32)).astype(bf16)


def nt(a, b):
    return lax.dot_general(a, b, (((1,), (1,)), ((), ())), preferred_element_type=f32)


def span_part(within, rate, radius, table):
    offs = iota_f((SPAN, LANES), 0) - HALO
    four = jnp.concatenate(factors(offs, within, rate, radius), axis=1)
    hi, lo = split(four)
    return jnp.dot(table, jnp.concatenate([hi, lo, hi], axis=0), preferred_element_type=f32)


def span_table(frequency, length):
    offs = iota_f((1, SPAN), 1) - HALO
    c, s = cos_sin(frequency * offs * (1.0 / length))
    hi, lo = split(jnp.concatenate([c, -s], axis=0))
    return jnp.concatenate([hi, hi, lo], axis=1)


class Sizes:
    def __init__(self, n_gx, n_gy, n_gz, pair_dev):
        self.n_gx, self.n_gy, self.n_gz = n_gx, n_gy, n_gz
        self.nx, self.ny, self.nz = CX * n_gx, CY * n_gy, CZ * n_gz
        self.nky, self.nkz = self.ny // n_gx, self.nz // (n_gy * n_gz)
        self.pair_dev = pair_dev
        self.per = LANES // pair_dev
        self.groups = n_gx // self.per
        self.wide = max(self.nx, LANES)
        self.kys = self.wide // self.nx
        self.blocks = self.nky // self.kys
        self.cols = 2 * self.nkz * n_gy
        self.rows = self.nky * self.nx


def kz_start(z, gy, gz, dy):
    block = lax.rem(gy + dy, z.n_gy) * z.n_gz + gz
    return (block * z.nkz).astype(f32)


def put3(ref, rows, k, hi, lo, order):
    for n, which in enumerate(order):
        ref[rows, n * DEPTH + k * LANES : n * DEPTH + (k + 1) * LANES] = lo if which else hi


def chunk_work(z, place, prm, ytab, ztab, s):
    gx, gy, gz = place
    row = lambda a: prm[a : a + 1, :]
    cx, cy, cz, ox, oy, oz, rate, radius = [row(COEFS + n) for n in range(8)]
    nky, nkz, nx = z.nky, z.nkz, z.nx

    kyc = iota_f((nky, 1), 0) + (gx * nky).astype(f32)
    part = span_part(oy, rate, radius, ytab[...])
    pc, ps = cos_sin(kyc * cy * (1.0 / z.ny))
    fy = []
    for d in range(SIDE):
        a = part[:nky, d * LANES : (d + 1) * LANES]
        b = part[nky:, d * LANES : (d + 1) * LANES]
        fy.append((a * pc + b * ps, b * pc - a * ps))

    fx = factors(wrapped(iota_f((nx, LANES), 0), cx, float(z.nx)), ox, rate, radius)
    for k in range(SIDE):
        for i in range(SIDE):
            re = im = None
            for j in range(SIDE):
                c = row((i * SIDE + j) * SIDE + k)
                re = c * fy[j][0] if re is None else re + c * fy[j][0]
                im = c * fy[j][1] if im is None else im + c * fy[j][1]
            s.h[k * SIDE + i, :nky] = re
            s.h[k * SIDE + i, nky:] = im

    fxl = factors(
        wrapped(iota_f((CX, LANES), 0) + (gx * CX).astype(f32), cx, float(z.nx)), ox, rate, radius
    )
    fyl = factors(
        iota_f((CYW, LANES), 0) + ((gy * CY).astype(f32) - HALO) - cy, oy, rate, radius
    )
    fzl = factors(
        wrapped(iota_f((CZ, LANES), 0) + (gz * CZ).astype(f32), cz, float(z.nz)), oz, rate, radius
    )
    for k in range(SIDE):
        for j in range(SIDE):
            v = None
            for i in range(SIDE):
                w = row((i * SIDE + j) * SIDE + k) * fxl[i]
                v = w if v is None else v + w
            s.hd[k * SIDE + j] = v
        hi, lo = split(fzl[k])
        put3(s.zd, slice(0, CZ), k, hi, lo, (0, 0, 1))

    part = span_part(oz, rate, radius, ztab[...])
    n = z.n_gy * nkz
    low = iota_f((8, 1), 0)
    cb, sb = cos_sin(low * cz * (1.0 / z.nz))
    heads = jnp.concatenate(
        [iota_f((nkz // 8, 1), 0) * 8.0 + kz_start(z, gy, gz, dy) for dy in range(z.n_gy)], axis=0
    )
    s.ea[0], s.ea[1] = cos_sin(heads * cz * (1.0 / z.nz))
    pcs, pss = [], []
    for a in range(n // 8):
        ca, sa = s.ea[0, a : a + 1, :], s.ea[1, a : a + 1, :]
        pcs.append(ca * cb - sa * sb)
        pss.append(sa * cb + ca * sb)
    pc, ps = jnp.concatenate(pcs, axis=0), jnp.concatenate(pss, axis=0)
    for k in range(SIDE):
        a = part[:n, k * LANES : (k + 1) * LANES]
        b = part[n:, k * LANES : (k + 1) * LANES]
        for dy in range(z.n_gy):
            for m, v in enumerate((a * pc + b * ps, b * pc - a * ps)):
                hi, lo = split(v[dy * nkz : (dy + 1) * nkz])
                start = (2 * dy + m) * nkz
                put3(s.z, slice(start, start + nkz), k, hi, lo, (0, 0, 1))

    def build_cells():
        for x in range(CX):
            for k in range(SIDE):
                v = None
                for j in range(SIDE):
                    w = s.hd[k * SIDE + j, x : x + 1, :] * fyl[j]
                    v = w if v is None else v + w
                hi, lo = split(v)
                put3(s.d, slice(x * CYW, (x + 1) * CYW), k, hi, lo, (0, 1, 0))

    def build(g):
        t = s.t.at[g % 2]
        for m in range(2):
            for kk in range(z.kys):
                r = m * nky + g * z.kys + kk
                o = m * z.wide + kk * nx
                for k in range(SIDE):
                    v = None
                    for i in range(SIDE):
                        w = s.h[k * SIDE + i, r : r + 1, :] * fx[i]
                        v = w if v is None else v + w
                    hi, lo = split(v)
                    put3(t, slice(o, o + nx), k, hi, lo, (0, 1, 0))

    def add_cells():
        more = nt(s.d[...], s.zd[...])
        s.dacc[...] = s.dacc[...] + more.reshape(CX, CYW, CZ)

    def add(g):
        rows = slice(2 * z.wide * g, 2 * z.wide * (g + 1))
        s.acc[rows] = s.acc[rows] + nt(s.t[g % 2], s.z[...])

    build_cells()
    late = add_cells
    for g in range(z.blocks):
        build(g)
        late()
        late = functools.partial(add, g)
    late()


class Scratch:
    pass


def params_of(z, cells, offs, e_index, r_index, exponents, pm):
    n = z.pair_dev
    pm[...] = jnp.zeros_like(pm)
    radius = (HALO - r_index[...]).astype(f32)
    chosen = None
    for e in range(exponents.shape[0]):
        w = jnp.where(e_index[...] == e, exponents[e], 0.0)
        chosen = w if chosen is None else chosen + w
    pm[0:3, :n] = cells[...].astype(f32)
    pm[3:6, :n] = offs[...]
    pm[6:7, :n] = chosen / (radius * radius)
    pm[7:8, :n] = radius


def coefficients(z, basis, blocks):
    bh, bl = split(basis[...])
    ph, pb = split(blocks[...])
    ph = jnp.concatenate([ph] * FOLD, axis=0)
    pb = jnp.concatenate([pb] * FOLD, axis=0)
    both = nt(bh, ph) + (nt(bh, pb) + nt(bl, ph))
    lane = lax.broadcasted_iota(jnp.int32, (TOP, FOLD * z.pair_dev), 1) // z.pair_dev
    v = both[:TOP]
    for g in range(1, FOLD):
        v = jnp.where(lane == g, both[g * TOP : (g + 1) * TOP], v)
    return v


def unpack(z, blocks, prm):
    owner = lax.broadcasted_iota(jnp.int32, (TOP, LANES), 1) // z.pair_dev
    for g in range(FOLD):
        v = None
        for d, block in enumerate(blocks):
            shift = (d - g) % FOLD * z.pair_dev
            w = block[:TOP]
            w = pltpu.roll(w, shift, 1) if shift else w
            v = w if v is None else jnp.where(owner == d, w, v)
        prm[g * TOP : (g + 1) * TOP] = v
    v = None
    for d, block in enumerate(blocks):
        w = block[TOP:]
        w = pltpu.roll(w, d * z.pair_dev, 1) if d else w
        v = w if v is None else jnp.where(owner[:8] == d, w, v)
    prm[COEFS : COEFS + 8] = v


def swapped(z, b):
    lane = lax.broadcasted_iota(jnp.int32, (b.shape[0], LANES), 1)
    first = lane % (2 * z.nkz) < z.nkz
    out = []
    for c in range(z.cols // LANES):
        w = b[:, c * LANES : (c + 1) * LANES]
        down = pltpu.roll(w, LANES - z.nkz, 1)
        up = down if 2 * z.nkz == LANES else pltpu.roll(w, z.nkz, 1)
        out.append(jnp.where(first, down, -up))
    return jnp.concatenate(out, axis=1)


def kernel(
    z, basis_hbm, blocks_hbm, cells_hbm, offs_hbm, ei_hbm, ri_hbm, ex_hbm, xt_hbm,
    own, got, dacc, edges,
    basis, blocks, cells, offs, e_index, r_index, exponents, xt, pm, prm, cols, give,
    h, hd, ea, acc,
    in_sem, send_z, recv_z, send_c, recv_c, send_e, recv_e, send_d, recv_d,
):
    n_gx, n_gy, n_gz = z.n_gx, z.n_gy, z.n_gz
    gx, gy, gz = (lax.axis_index(a) for a in ("gx", "gy", "gz"))
    place = gx, gy, gz
    mesh_type = pl.DeviceIdType.MESH

    def along_z(r):
        return gx, gy, lax.rem(gz + n_gz - r, n_gz)

    def along_x(dx):
        return lax.rem(gx + n_gx - dx, n_gx), gy, gz

    def along_y(dy):
        return gx, lax.rem(gy + n_gy + dy, n_gy), gz

    barrier = pltpu.get_barrier_semaphore()
    for r in range(1, n_gz):
        pl.semaphore_signal(barrier, inc=1, device_id=along_z(r), device_id_type=mesh_type)

    def greet(dx, carry):
        pl.semaphore_signal(barrier, inc=1, device_id=along_x(dx), device_id_type=mesh_type)
        return carry

    lax.fori_loop(1, n_gx, greet, 0)
    for dy in range(1, n_gy):
        pl.semaphore_signal(barrier, inc=1, device_id=along_y(dy), device_id_type=mesh_type)

    pairs = [
        (blocks_hbm, blocks), (basis_hbm, basis), (cells_hbm, cells), (offs_hbm, offs),
        (ei_hbm, e_index), (ri_hbm, r_index), (ex_hbm, exponents), (xt_hbm, xt),
    ]
    loads = [
        pltpu.make_async_copy(a, b, in_sem.at[n]) for n, (a, b) in enumerate(pairs)
    ]
    for c in loads:
        c.start()
    for c in loads[:-1]:
        c.wait()
    params_of(z, cells, offs, e_index, r_index, exponents, pm)
    cols[0, 0, :TOP] = coefficients(z, basis, blocks)
    cols[0, 0, TOP:] = pm[...]

    def body(ytab, ztab, t, zs, d, zd):
        s = Scratch()
        s.t, s.z, s.d, s.zd, s.h, s.hd, s.ea, s.acc, s.dacc = t, zs, d, zd, h, hd, ea, acc, dacc
        kyc = iota_f((z.nky, 1), 0) + (gx * z.nky).astype(f32)
        kzc = jnp.concatenate(
            [iota_f((z.nkz, 1), 0) + kz_start(z, gy, gz, dy) for dy in range(n_gy)], axis=0
        )
        ytab[...] = span_table(kyc, z.ny)
        ztab[...] = span_table(kzc, z.nz)
        for ref in (acc, dacc):
            ref[...] = jnp.zeros_like(ref)
        pl.semaphore_wait(barrier, n_gz + n_gx + n_gy - 3)

        def copy_z(r):
            return pltpu.make_async_remote_copy(
                src_ref=cols.at[0, 0],
                dst_ref=cols.at[r, 0],
                send_sem=send_z.at[r],
                recv_sem=recv_z.at[r],
                device_id=along_z(r),
                device_id_type=mesh_type,
            )

        def copy_c(r, dx):
            return pltpu.make_async_remote_copy(
                src_ref=cols.at[r, 0],
                dst_ref=cols.at[r, dx],
                send_sem=send_c.at[r * n_gx + dx],
                recv_sem=recv_c.at[r * n_gx + dx],
                device_id=along_x(dx),
                device_id_type=mesh_type,
            )

        def forward(r):
            def one(dx, carry):
                copy_c(r, dx).start()
                return carry

            lax.fori_loop(1, n_gx, one, 0)

        for r in range(1, n_gz):
            copy_z(r).start()
        forward(0)
        for r in range(1, n_gz - 1):
            copy_z(r).wait_recv()
            forward(r)

        def step(c, carry):
            r, g = c // z.groups, c % z.groups

            @pl.when(c == z.groups)
            def _():
                copy_z(n_gz - 1).wait_recv()
                forward(n_gz - 1)

            for d in range(z.per):
                dx = g * z.per + d

                @pl.when(dx > 0)
                def _(dx=dx):
                    copy_c(r, dx).wait_recv()

            unpack(z, [cols[r, g * z.per + d] for d in range(z.per)], prm)
            chunk_work(z, place, prm, ytab, ztab, s)
            return carry

        lax.fori_loop(0, n_gz * z.groups, step, 0)

        def copy_d(which):
            return pltpu.make_async_remote_copy(
                src_ref=dacc.at[:, pl.ds(which * (CY + HALO), HALO), :],
                dst_ref=edges.at[which],
                send_sem=send_d.at[which],
                recv_sem=recv_d.at[which],
                device_id=along_y(2 * which - 1),
                device_id_type=mesh_type,
            )

        def copy_e(dy, g):
            rows = pl.ds(g * z.wide, z.wide)
            return pltpu.make_async_remote_copy(
                src_ref=give.at[dy - 1, rows],
                dst_ref=got.at[dy - 1, rows],
                send_sem=send_e.at[dy * z.blocks + g],
                recv_sem=recv_e.at[dy * z.blocks + g],
                device_id=along_y(dy),
                device_id_type=mesh_type,
            )

        loads[-1].wait()
        for g in range(z.blocks):
            hi, lo = split(acc[2 * z.wide * g : 2 * z.wide * (g + 1)])
            q = jnp.dot(
                xt[...], jnp.concatenate([hi, lo, hi], axis=0), preferred_element_type=f32
            )
            out = q[: z.wide] + swapped(z, q[z.wide :])
            rows = slice(g * z.wide, (g + 1) * z.wide)
            own[rows] = out[:, : 2 * z.nkz]
            for dy in range(1, n_gy):
                give[dy - 1, rows] = out[:, 2 * z.nkz * dy : 2 * z.nkz * (dy + 1)]
            if g == 0:
                for which in range(2):
                    copy_d(which).start()
            else:
                for dy in range(1, n_gy):
                    copy_e(dy, g - 1).start()
        for dy in range(1, n_gy):
            copy_e(dy, z.blocks - 1).start()
        for r in range(1, n_gz):
            copy_z(r).wait_send()

        def drain(c, carry):
            @pl.when(c % n_gx > 0)
            def _():
                copy_c(c // n_gx, c % n_gx).wait_send()

            return carry

        lax.fori_loop(0, n_gz * n_gx, drain, 0)
        for which in range(2):
            copy_d(which).wait()
        for g in range(z.blocks):
            for dy in range(1, n_gy):
                copy_e(dy, g).wait()

    pl.run_scoped(
        body,
        pltpu.VMEM((2 * z.nky, 3 * SPAN), bf16),
        pltpu.VMEM((z.cols, 3 * SPAN), bf16),
        pltpu.VMEM((2, 2 * z.wide, 3 * DEPTH), bf16),
        pltpu.VMEM((z.cols, 3 * DEPTH), bf16),
        pltpu.VMEM((CX * CYW, 3 * DEPTH), bf16),
        pltpu.VMEM((CZ, 3 * DEPTH), bf16),
    )


def finish(z, own, got, dacc, edges, dens_ref, spec_ref):
    total = own[...]
    for dy in range(1, z.n_gy):
        total = total + got[dy - 1]
    spec_ref[0] = total[:, : z.nkz]
    spec_ref[1] = total[:, z.nkz :]
    dens_ref[...] = dacc[:, HALO : HALO + CY]
    dens_ref[:, CY - HALO :] = dens_ref[:, CY - HALO :] + edges[0]
    dens_ref[:, :HALO] = dens_ref[:, :HALO] + edges[1]


def x_table(z):
    idx = np.arange(z.nx)
    angle = (idx[:, None] * idx[None, :] % z.nx) * (2.0 * math.pi / z.nx)
    eye = np.eye(z.kys)
    c, s = np.kron(eye, np.cos(angle)), np.kron(eye, np.sin(angle))
    full = np.block([[c, s], [s, -c]]) / math.sqrt(z.nx * z.ny * z.nz)
    full = full.astype(np.float32)
    hi = full.astype(ml_dtypes.bfloat16)
    lo = (full - hi.astype(np.float32)).astype(ml_dtypes.bfloat16)
    return np.concatenate([hi, hi, lo], axis=1)


def shards(
    pair_blocks, basis_map, pair_cells, pair_offsets, exponent_index, radius_index, exponents
):
    n_gx, n_gy, n_gz = (lax.axis_size(a) for a in ("gx", "gy", "gz"))
    pair_dev = pair_blocks.shape[1]
    z = Sizes(n_gx, n_gy, n_gz, pair_dev)
    assert FOLD * pair_dev == LANES and n_gx % z.per == 0 and n_gz >= 3 and n_gy >= 2
    in_vmem = pl.BlockSpec(memory_space=pltpu.VMEM)
    in_hbm = pl.BlockSpec(memory_space=pl.ANY)
    basis = basis_map.T
    blocks = pair_blocks.T
    xt = jnp.asarray(x_table(z))
    ei, ri = exponent_index.reshape(1, -1), radius_index.reshape(1, -1)
    dma = pltpu.SemaphoreType.DMA
    own, got, dacc, edges = pl.pallas_call(
        functools.partial(kernel, z),
        out_shape=[
            jax.ShapeDtypeStruct((z.rows, 2 * z.nkz), f32),
            jax.ShapeDtypeStruct((n_gy - 1, z.rows, 2 * z.nkz), f32),
            jax.ShapeDtypeStruct((CX, CYW, CZ), f32),
            jax.ShapeDtypeStruct((2, CX, HALO, CZ), f32),
        ],
        in_specs=[in_hbm] * 8,
        out_specs=[in_vmem] * 4,
        scratch_shapes=[
            pltpu.VMEM(basis.shape, f32),
            pltpu.VMEM(blocks.shape, f32),
            pltpu.VMEM(pair_cells.shape, jnp.int32),
            pltpu.VMEM(pair_offsets.shape, f32),
            pltpu.VMEM(ei.shape, jnp.int32),
            pltpu.VMEM(ri.shape, jnp.int32),
            pltpu.SMEM(exponents.shape, f32),
            pltpu.VMEM(xt.shape, bf16),
            pltpu.VMEM((8, LANES), f32),
            pltpu.VMEM((COEFS + 8, LANES), f32),
            pltpu.VMEM((n_gz, n_gx, BLOCK_ROWS, LANES), f32),
            pltpu.VMEM((n_gy - 1, z.rows, 2 * z.nkz), f32),
            pltpu.VMEM((SIDE * SIDE, 2 * z.nky, LANES), f32),
            pltpu.VMEM((SIDE * SIDE, CX, LANES), f32),
            pltpu.VMEM((2, n_gy * z.nkz // 8, LANES), f32),
            pltpu.VMEM((2 * z.rows, z.cols), f32),
            dma((8,)),
            dma((n_gz,)),
            dma((n_gz,)),
            dma((n_gz * n_gx,)),
            dma((n_gz * n_gx,)),
            dma((n_gy * z.blocks,)),
            dma((n_gy * z.blocks,)),
            dma((2,)),
            dma((2,)),
        ],
        compiler_params=pltpu.CompilerParams(
            collective_id=0, has_side_effects=True, vmem_limit_bytes=VMEM_LIMIT
        ),
    )(basis, blocks, pair_cells, pair_offsets, ei, ri, exponents, xt)
    dens, spec = pl.pallas_call(
        functools.partial(finish, z),
        out_shape=[
            jax.ShapeDtypeStruct((CX, CY, CZ), f32),
            jax.ShapeDtypeStruct((2, z.rows, z.nkz), f32),
        ],
        in_specs=[in_vmem] * 4,
        out_specs=[in_vmem] * 2,
        compiler_params=pltpu.CompilerParams(vmem_limit_bytes=VMEM_LIMIT),
    )(own, got, dacc, edges)
    return dens, spec.reshape(2, z.nky, z.nx, z.nkz).transpose(0, 3, 1, 2)


def solution(mesh):
    placed = (
        P(None, ("gx", "gy", "gz")),
        P(),
        P(None, ("gx", "gy", "gz")),
        P(None, ("gx", "gy", "gz")),
        P(("gx", "gy", "gz")),
        P(("gx", "gy", "gz")),
        P(),
    )
    return jax.shard_map(
        shards,
        mesh=mesh,
        in_specs=placed,
        out_specs=(P("gx", "gy", "gz"), P(None, ("gy", "gz"), "gx", None)),
        check_vma=False,
    )
```

time: 32.7 us -> 26.4 us (0.81)
  Pallas kernels: 29 us -> 22 us
  local copies, waits for them, and re-layouts: 0.73 us -> 3.47 us
  matrix products: 1.17 us -> 0 us
  other arithmetic: 0.89 us -> 0 us
    pallas_call x2, Pallas kernels: 29 us -> 22 us  [the longest x1 21 us: shards(): pl.pallas_call(functools.partial(kernel, z), out_shape=[jax.ShapeDtypeStr...]
    unnamed x10 -> x16, local copies, waits for them, and re-layouts: 0.62 us -> 3.47 us
    dot_general x1 -> x0, matrix products: 1.17 us -> none  [shards(): coefs = jnp.dot(basis_map.T, pair_blocks, precision=highest)]
    reduce_sum x1 -> x0, other arithmetic: 0.8 us -> none  [shards(): rate = jnp.sum(exponents[:, None] * selector, axis=0) / (radius * radius)]
where the time goes in v1:
time: 26.4 us; the launch traced here: 26.1 us
  Pallas kernels  22 us (83%)
  local copies, waits for them, and re-layouts  3.47 us (13%)
  between operations  0.69 us (3%)
    pallas_call x1, Pallas kernels, shards(): pl.pallas_call(functools.partial(kernel, z), out_shape=[jax.ShapeDtypeStr...  21 us
    unnamed x16, local copies, waits for them, and re-layouts  3.47 us
    pallas_call x1, Pallas kernels, shards(): pl.pallas_call(functools.partial(finish, z), out_shape=[jax.ShapeDtypeStr...  0.94 us

profile of v1, /device:TPU:0, one launch (start us, length us, event | category | flops | bytes accessed | tf_op | source)
XLA Modules:
  0.0 26.1 jit_solution(809830648551596429)
XLA Ops:
  0.6 0.0 copy-start.4
  0.6 0.0 copy-start.3
  0.7 0.0 copy-start.5
  0.7 0.0 copy-start.6
  0.7 0.0 copy-start.7
  0.7 0.6 %copy-done.4 = f32[3,32]{1,0:T(4,128)S(1)} copy-done((f32[3,32]{1,0:T(4,128)S(1)}, f32[3,32]{1,0:T(4,128)}, u32[]{:S(2)}) %copy-start.4) | copy-done | bytes 408
  1.3 0.0 copy-done.3
  1.3 0.0 copy-done.5
  1.3 0.0 copy-done.6
  1.3 0.0 copy-done.7
  1.4 0.0 copy-start
  1.4 1.0 %copy-done = bf16[256,768]{1,0:T(8,128)(2,1)S(1)} copy-done((bf16[256,768]{1,0:T(8,128)(2,1)S(1)}, bf16[256,768]{1,0:T(8,128)(2,1)}, u32[]{:S(2)}) %copy-start) | copy-done | bytes 393240
  2.3 0.0 copy-start.1
  2.4 0.9 %copy-done.1 = f32[529,64]{0,1:T(8,128)S(1)} copy-done((f32[529,64]{0,1:T(8,128)S(1)}, f32[529,64]{0,1:T(8,128)}, u32[]{:S(2)}) %copy-start.1) | copy-done | bytes 135448
  3.3 0.0 copy-start.2
  3.3 0.9 %copy-done.2 = f32[529,32]{0,1:T(8,128)S(1)} copy-done((f32[529,32]{0,1:T(8,128)S(1)}, f32[529,32]{0,1:T(8,128)}, u32[]{:S(2)}) %copy-start.2) | copy-done | bytes 67736
  4.2 21.0 %shard_map.95 = (f32[512,128]{1,0:T(8,128)S(1)}, f32[1,512,128]{2,1,0:T(8,128)S(1)}, f32[8,48,128]{2,1,0:T(8,128)S(1)}, f32[2,8,8,128]{3,2,1,0:T(8,128)S(1)}) custom-call(f32[64,529]{1,0:T(8,128)S(1)} %bitcast.7, f32[32,529]{1,0:T(8,128)S(1)} %bitcast.8, s32[3,32]{1,0:T(4,128)S(1)} %copy-done.3, f32[3,32]{1,0:T(4,128)S(1)} %copy-done.4, ...), custom_call_target="tpu_custom_call" | custom-call | tf_op jit(solution)/shard_map/pallas_call | solution.py:508
  25.2 0.9 %shard_map.96 = (f32[8,32,128]{2,1,0:T(8,128)}, f32[2,512,64]{2,1,0:T(8,128)}) custom-call(f32[512,128]{1,0:T(8,128)S(1)} %get-tuple-element.8.own, f32[1,512,128]{2,1,0:T(8,128)S(1)} %get-tuple-element.9.got, f32[8,48,128]{2,1,0:T(8,128)S(1)} %get-tuple-element.10.dacc, f32[2,8,8,128]{3,2,1,0:T(8,128)S(1)} %get-tuple-element.11.edges), custom_call_target="tpu_custom_call" | custom-call | tf_op jit(solution)/shard_map/pallas_call | solution.py:549
Async XLA Ops:
  0.6 0.7 %copy-start.4 = (f32[3,32]{1,0:T(4,128)S(1)}, f32[3,32]{1,0:T(4,128)}, u32[]{:S(2)}) copy-start(f32[3,32]{1,0:T(4,128)} %offs_hbm.1) | copy-start | bytes 1156
  0.6 0.7 %copy-start.3 = (s32[3,32]{1,0:T(4,128)S(1)}, s32[3,32]{1,0:T(4,128)}, u32[]{:S(2)}) copy-start(s32[3,32]{1,0:T(4,128)} %cells_hbm.1) | copy-start | bytes 1156
  0.7 0.7 %copy-start.5 = (s32[32]{0:T(128)S(1)}, s32[32]{0:T(128)}, u32[]{:S(2)}) copy-start(s32[32]{0:T(128)} %param.12) | copy-start | bytes 388
  0.7 0.7 %copy-start.6 = (s32[32]{0:T(128)S(1)}, s32[32]{0:T(128)}, u32[]{:S(2)}) copy-start(s32[32]{0:T(128)} %param.13) | copy-start | bytes 388
  0.7 0.7 %copy-start.7 = (f32[16]{0:T(128)S(1)}, f32[16]{0:T(128)}, u32[]{:S(2)}) copy-start(f32[16]{0:T(128)} %ex_hbm.1) | copy-start | bytes 196
  1.4 1.0 %copy-start = (bf16[256,768]{1,0:T(8,128)(2,1)S(1)}, bf16[256,768]{1,0:T(8,128)(2,1)}, u32[]{:S(2)}) copy-start(bf16[256,768]{1,0:T(8,128)(2,1)} %constant.2.clone.xt_hbm) | copy-start | bytes 1179652
  2.3 0.9 %copy-start.1 = (f32[529,64]{0,1:T(8,128)S(1)}, f32[529,64]{0,1:T(8,128)}, u32[]{:S(2)}) copy-start(f32[529,64]{0,1:T(8,128)} %param.9) | copy-start | bytes 406276
  3.3 0.9 %copy-start.2 = (f32[529,32]{0,1:T(8,128)S(1)}, f32[529,32]{0,1:T(8,128)}, u32[]{:S(2)}) copy-start(f32[529,32]{0,1:T(8,128)} %param.8) | copy-start | bytes 203140

commit v2 on v1

--- a/solution.py
+++ b/solution.py
@@ -499,7 +499,7 @@
     z = Sizes(n_gx, n_gy, n_gz, pair_dev)
     assert FOLD * pair_dev == LANES and n_gx % z.per == 0 and n_gz >= 3 and n_gy >= 2
     in_vmem = pl.BlockSpec(memory_space=pltpu.VMEM)
-    in_hbm = pl.BlockSpec(memory_space=pl.ANY)
+    in_hbm = pl.BlockSpec(memory_space=pltpu.HBM)
     basis = basis_map.T
     blocks = pair_blocks.T
     xt = jnp.asarray(x_table(z))
@@ -545,7 +545,12 @@
         compiler_params=pltpu.CompilerParams(
             collective_id=0, has_side_effects=True, vmem_limit_bytes=VMEM_LIMIT
         ),
-    )(basis, blocks, pair_cells, pair_offsets, ei, ri, exponents, xt)
+    )(
+        *(
+            pltpu.with_memory_space_constraint(a, pltpu.HBM)
+            for a in (basis, blocks, pair_cells, pair_offsets, ei, ri, exponents, xt)
+        )
+    )
     dens, spec = pl.pallas_call(
         functools.partial(finish, z),
         out_shape=[

time: 26.4 us -> 22.8 us (0.86)
  local copies, waits for them, and re-layouts: 3.47 us -> 0 us
    unnamed x16 -> x0, local copies, waits for them, and re-layouts: 3.47 us -> none
where the time goes in v2:
time: 22.8 us; the launch traced here: 22.7 us
  Pallas kernels  22 us (96%)
  between operations  0.64 us (3%)
    pallas_call x1, Pallas kernels, shards(): pl.pallas_call(functools.partial(kernel, z), out_shape=[jax.ShapeDtypeStr...  21.1 us
    pallas_call x1, Pallas kernels, shards(): pl.pallas_call(functools.partial(finish, z), out_shape=[jax.ShapeDtypeStr...  0.93 us

profile of v2, /device:TPU:0, one launch (start us, length us, event | category | flops | bytes accessed | tf_op | source)
XLA Modules:
  0.0 22.7 jit_solution(11721903213690261833)
XLA Ops:
  0.6 21.1 %shard_map.95 = (f32[512,128]{1,0:T(8,128)S(1)}, f32[1,512,128]{2,1,0:T(8,128)S(1)}, f32[8,48,128]{2,1,0:T(8,128)S(1)}, f32[2,8,8,128]{3,2,1,0:T(8,128)S(1)}) custom-call(f32[64,529]{1,0:T(8,128)} %bitcast.7, f32[32,529]{1,0:T(8,128)} %bitcast.8, s32[3,32]{1,0:T(4,128)} %cells_hbm.1, f32[3,32]{1,0:T(4,128)} %offs_hbm.1, s32[1,32]{1,0:T(1,128)} %bitcast.9, ...), custom_call_target="tpu_custom_call" | custom-call | tf_op jit(solution)/shard_map/pallas_call | solution.py:508
  21.7 0.9 %shard_map.96 = (f32[8,32,128]{2,1,0:T(8,128)}, f32[2,512,64]{2,1,0:T(8,128)}) custom-call(f32[512,128]{1,0:T(8,128)S(1)} %get-tuple-element.8.own, f32[1,512,128]{2,1,0:T(8,128)S(1)} %get-tuple-element.9.got, f32[8,48,128]{2,1,0:T(8,128)S(1)} %get-tuple-element.10.dacc, f32[2,8,8,128]{3,2,1,0:T(8,128)S(1)} %get-tuple-element.11.edges), custom_call_target="tpu_custom_call" | custom-call | tf_op jit(solution)/shard_map/pallas_call | solution.py:554

commit v3 on v2

--- a/solution.py
+++ b/solution.py
@@ -17,13 +17,14 @@
 CZ = 128
 SIDE = DEG + 1
 LANES = 128
-SPAN = 32
 VMEM_LIMIT = 40 << 20
 COEFS = SIDE**3
 FOLD = 4
 TOP = COEFS // FOLD
 BLOCK_ROWS = TOP + 8
 CYW = CY + 2 * HALO
+CZW = CZ + 2 * HALO
+TS = 4
 DEPTH = SIDE * LANES
 
 f32 = jnp.float32
@@ -56,9 +57,9 @@
     return jnp.where(d > total - 1 - HALO, d - total, d)
 
 
-def factors(offset, within, rate, radius):
+def factors(offset, within, fall, radius):
     u = offset - within
-    env = jnp.where(jnp.abs(offset) <= radius, jnp.exp(-rate * u * u), 0.0)
+    env = jnp.where(jnp.abs(offset) <= radius, jnp.exp2(fall * (u * u)), 0.0)
     s = u * (1.0 / HALO)
     out = [env]
     for _ in range(DEG):
@@ -73,20 +74,6 @@
 
 def nt(a, b):
     return lax.dot_general(a, b, (((1,), (1,)), ((), ())), preferred_element_type=f32)
-
-
-def span_part(within, rate, radius, table):
-    offs = iota_f((SPAN, LANES), 0) - HALO
-    four = jnp.concatenate(factors(offs, within, rate, radius), axis=1)
-    hi, lo = split(four)
-    return jnp.dot(table, jnp.concatenate([hi, lo, hi], axis=0), preferred_element_type=f32)
-
-
-def span_table(frequency, length):
-    offs = iota_f((1, SPAN), 1) - HALO
-    c, s = cos_sin(frequency * offs * (1.0 / length))
-    hi, lo = split(jnp.concatenate([c, -s], axis=0))
-    return jnp.concatenate([hi, hi, lo], axis=1)
 
 
 class Sizes:
@@ -104,9 +91,50 @@
         self.rows = self.nky * self.nx
 
 
-def kz_start(z, gy, gz, dy):
-    block = lax.rem(gy + dy, z.n_gy) * z.n_gz + gz
-    return (block * z.nkz).astype(f32)
+def source_z(z, gz, r):
+    step = jnp.where(gz < z.n_gz // 2, r, z.n_gz - r)
+    return lax.rem(gz + step, z.n_gz)
+
+
+def kz_of(z, gy, gz):
+    starts = []
+    for dy in range(z.n_gy):
+        block = lax.rem(gy + dy, z.n_gy) * z.n_gz + gz
+        starts.append(iota_f((z.nkz, 1), 0) + (block * z.nkz).astype(f32))
+    return jnp.concatenate(starts, axis=0)
+
+
+def paired(z, a, b):
+    n = z.nkz
+    out = []
+    for dy in range(z.n_gy):
+        out += [a[dy * n : (dy + 1) * n], b[dy * n : (dy + 1) * n]]
+    return jnp.concatenate(out, axis=0)
+
+
+def z_tables(z, place, ztab):
+    gx, gy, gz = place
+    kz = kz_of(z, gy, gz)
+    col = lax.broadcasted_iota(jnp.int32, (1, CZW), 1)
+    cell = jnp.where(col < CZ + HALO, col, col - CZW).astype(f32)
+    c0, s0 = cos_sin(kz * cell * (1.0 / z.nz))
+    for r in range(z.n_gz):
+        source = source_z(z, gz, r).astype(f32)
+        ca, sa = cos_sin(kz * source * (1.0 / z.n_gz))
+        c = c0 * ca - s0 * sa
+        s = s0 * ca + c0 * sa
+        hi, lo = split(paired(z, c, -s))
+        ztab[r] = jnp.concatenate([hi, hi, lo], axis=1)
+
+
+def y_table(z, place, ytab):
+    gx, gy, gz = place
+    row = lax.broadcasted_iota(jnp.int32, (2 * z.nky, 1), 0)
+    ky = (row // (2 * z.kys) * z.kys + row % z.kys + gx * z.nky).astype(f32)
+    y = iota_f((1, CYW), 1) + ((gy * CY).astype(f32) - HALO)
+    c, s = cos_sin(ky * y * (1.0 / z.ny))
+    hi, lo = split(jnp.where(row % (2 * z.kys) < z.kys, c, -s))
+    ytab[...] = jnp.concatenate([hi, hi, lo], axis=1)
 
 
 def put3(ref, rows, k, hi, lo, order):
@@ -114,40 +142,39 @@
         ref[rows, n * DEPTH + k * LANES : n * DEPTH + (k + 1) * LANES] = lo if which else hi
 
 
-def chunk_work(z, place, prm, ytab, ztab, s):
+def stack3(ref, k, v):
+    hi, lo = split(v)
+    n = v.shape[0]
+    lanes = slice(k * LANES, (k + 1) * LANES)
+    ref[:n, lanes] = hi
+    ref[n : 2 * n, lanes] = lo
+    ref[2 * n :, lanes] = hi
+
+
+def chunk_work(z, place, r, prm, s, after=None):
     gx, gy, gz = place
     row = lambda a: prm[a : a + 1, :]
     cx, cy, cz, ox, oy, oz, rate, radius = [row(COEFS + n) for n in range(8)]
-    nky, nkz, nx = z.nky, z.nkz, z.nx
-
-    kyc = iota_f((nky, 1), 0) + (gx * nky).astype(f32)
-    part = span_part(oy, rate, radius, ytab[...])
-    pc, ps = cos_sin(kyc * cy * (1.0 / z.ny))
-    fy = []
-    for d in range(SIDE):
-        a = part[:nky, d * LANES : (d + 1) * LANES]
-        b = part[nky:, d * LANES : (d + 1) * LANES]
-        fy.append((a * pc + b * ps, b * pc - a * ps))
-
-    fx = factors(wrapped(iota_f((nx, LANES), 0), cx, float(z.nx)), ox, rate, radius)
+    fall = rate * (-1.0 / math.log(2.0))
+    nx = z.nx
+
+    fy = factors(iota_f((CYW, LANES), 0) + ((gy * CY).astype(f32) - HALO) - cy, oy, fall, radius)
+    for j in range(SIDE):
+        s.fy[j] = fy[j]
+        stack3(s.yw, j, fy[j])
+    part = jnp.dot(s.ytab[...], s.yw[...], preferred_element_type=f32)
     for k in range(SIDE):
         for i in range(SIDE):
-            re = im = None
+            v = None
             for j in range(SIDE):
-                c = row((i * SIDE + j) * SIDE + k)
-                re = c * fy[j][0] if re is None else re + c * fy[j][0]
-                im = c * fy[j][1] if im is None else im + c * fy[j][1]
-            s.h[k * SIDE + i, :nky] = re
-            s.h[k * SIDE + i, nky:] = im
-
+                w = row((i * SIDE + j) * SIDE + k) * part[:, j * LANES : (j + 1) * LANES]
+                v = w if v is None else v + w
+            for g in range(z.blocks):
+                s.h[k * SIDE + i, g] = v[2 * z.kys * g : 2 * z.kys * (g + 1)]
+
+    fx = factors(wrapped(iota_f((nx, LANES), 0), cx, float(z.nx)), ox, fall, radius)
     fxl = factors(
-        wrapped(iota_f((CX, LANES), 0) + (gx * CX).astype(f32), cx, float(z.nx)), ox, rate, radius
-    )
-    fyl = factors(
-        iota_f((CYW, LANES), 0) + ((gy * CY).astype(f32) - HALO) - cy, oy, rate, radius
-    )
-    fzl = factors(
-        wrapped(iota_f((CZ, LANES), 0) + (gz * CZ).astype(f32), cz, float(z.nz)), oz, rate, radius
+        wrapped(iota_f((CX, LANES), 0) + (gx * CX).astype(f32), cx, float(z.nx)), ox, fall, radius
     )
     for k in range(SIDE):
         for j in range(SIDE):
@@ -156,71 +183,82 @@
                 w = row((i * SIDE + j) * SIDE + k) * fxl[i]
                 v = w if v is None else v + w
             s.hd[k * SIDE + j] = v
-        hi, lo = split(fzl[k])
-        put3(s.zd, slice(0, CZ), k, hi, lo, (0, 0, 1))
-
-    part = span_part(oz, rate, radius, ztab[...])
-    n = z.n_gy * nkz
-    low = iota_f((8, 1), 0)
-    cb, sb = cos_sin(low * cz * (1.0 / z.nz))
-    heads = jnp.concatenate(
-        [iota_f((nkz // 8, 1), 0) * 8.0 + kz_start(z, gy, gz, dy) for dy in range(z.n_gy)], axis=0
-    )
-    s.ea[0], s.ea[1] = cos_sin(heads * cz * (1.0 / z.nz))
-    pcs, pss = [], []
-    for a in range(n // 8):
-        ca, sa = s.ea[0, a : a + 1, :], s.ea[1, a : a + 1, :]
-        pcs.append(ca * cb - sa * sb)
-        pss.append(sa * cb + ca * sb)
-    pc, ps = jnp.concatenate(pcs, axis=0), jnp.concatenate(pss, axis=0)
+
+    cell = lax.broadcasted_iota(jnp.int32, (CZW, LANES), 0)
+    cell = jnp.where(cell < CZ + HALO, cell, cell - CZW).astype(f32)
+    source = source_z(z, gz, r) * CZ
+    fz = factors(cell - (cz - source.astype(f32)), oz, fall, radius)
     for k in range(SIDE):
-        a = part[:n, k * LANES : (k + 1) * LANES]
-        b = part[n:, k * LANES : (k + 1) * LANES]
-        for dy in range(z.n_gy):
-            for m, v in enumerate((a * pc + b * ps, b * pc - a * ps)):
-                hi, lo = split(v[dy * nkz : (dy + 1) * nkz])
-                start = (2 * dy + m) * nkz
-                put3(s.z, slice(start, start + nkz), k, hi, lo, (0, 0, 1))
-
-    def build_cells():
+        s.fe[0, k] = fz[k][CZ + HALO :]
+        s.fe[1, k] = fz[k][CZ : CZ + HALO]
+        stack3(s.zw, k, fz[k])
+    for k in range(SIDE):
+        lanes = slice(k * LANES, (k + 1) * LANES)
+        v = jnp.dot(s.ztab[r], s.zw[:, lanes], preferred_element_type=f32)
+        hi, lo = split(v)
+        put3(s.z, slice(0, z.cols), k, hi, lo, (0, 0, 1))
+
+    def cells():
         for x in range(CX):
             for k in range(SIDE):
                 v = None
                 for j in range(SIDE):
-                    w = s.hd[k * SIDE + j, x : x + 1, :] * fyl[j]
+                    w = s.hd[k * SIDE + j, x : x + 1, :] * s.fy[j]
                     v = w if v is None else v + w
                 hi, lo = split(v)
                 put3(s.d, slice(x * CYW, (x + 1) * CYW), k, hi, lo, (0, 1, 0))
+        hi, lo = s.zw[:CZ], s.zw[CZW : CZW + CZ]
+        more = nt(s.d[...], jnp.concatenate([hi, hi, lo], axis=1))
+        s.dacc[...] = s.dacc[...] + more.reshape(CX, CYW, CZ)
+
+    def edge(which):
+        for x in range(0, CX, 2):
+            for j in range(SIDE):
+                both = []
+                for xx in (x, x + 1):
+                    v = None
+                    for k in range(SIDE):
+                        w = s.hd[k * SIDE + j, xx : xx + 1, :] * s.fe[which, k]
+                        v = w if v is None else v + w
+                    both.append(v)
+                hi, lo = split(jnp.concatenate(both, axis=0))
+                put3(s.te, slice(x * HALO, (x + 2) * HALO), j, hi, lo, (0, 0, 1))
+        hi, lo = s.yw[:CYW], s.yw[CYW : 2 * CYW]
+        more = nt(jnp.concatenate([hi, lo, hi], axis=1), s.te[...])
+        s.eacc[which] = s.eacc[which] + more
 
     def build(g):
-        t = s.t.at[g % 2]
         for m in range(2):
             for kk in range(z.kys):
-                r = m * nky + g * z.kys + kk
                 o = m * z.wide + kk * nx
                 for k in range(SIDE):
                     v = None
                     for i in range(SIDE):
-                        w = s.h[k * SIDE + i, r : r + 1, :] * fx[i]
+                        q = m * z.kys + kk
+                        w = s.h[k * SIDE + i, g, q : q + 1, :] * fx[i]
                         v = w if v is None else v + w
                     hi, lo = split(v)
-                    put3(t, slice(o, o + nx), k, hi, lo, (0, 1, 0))
-
-    def add_cells():
-        more = nt(s.d[...], s.zd[...])
-        s.dacc[...] = s.dacc[...] + more.reshape(CX, CYW, CZ)
-
-    def add(g):
+                    put3(s.t[g % TS], slice(o, o + nx), k, hi, lo, (0, 1, 0))
+
+    def product(g):
         rows = slice(2 * z.wide * g, 2 * z.wide * (g + 1))
-        s.acc[rows] = s.acc[rows] + nt(s.t[g % 2], s.z[...])
-
-    build_cells()
-    late = add_cells
-    for g in range(z.blocks):
+        s.acc[rows] = s.acc[rows] + nt(s.t[g % TS][...], s.z[...])
+
+    near = jnp.where(gz < z.n_gz // 2, 0, 1)
+    if after is not None:
+        edge(1 - near)
+        add_edges(s.dacc, s.eacc)
+    build(0)
+    for g in range(1, z.blocks):
         build(g)
-        late()
-        late = functools.partial(add, g)
-    late()
+        product(g - 1)
+    product(z.blocks - 1)
+    if after is not None:
+        return
+    pl.when(r == 0)(cells)
+    pl.when(r == 1)(lambda: edge(near))
+    if z.groups > 1:
+        pl.when(r == z.n_gz - 1)(lambda: edge(1 - near))
 
 
 class Scratch:
@@ -288,8 +326,8 @@
     z, basis_hbm, blocks_hbm, cells_hbm, offs_hbm, ei_hbm, ri_hbm, ex_hbm, xt_hbm,
     own, got, dacc, edges,
     basis, blocks, cells, offs, e_index, r_index, exponents, xt, pm, prm, cols, give,
-    h, hd, ea, acc,
-    in_sem, send_z, recv_z, send_c, recv_c, send_e, recv_e, send_d, recv_d,
+    h, hd, fy, fe, acc, eacc,
+    ready, in_sem, send_z, recv_z, send_c, recv_c, send_e, recv_e, send_d, recv_d,
 ):
     n_gx, n_gy, n_gz = z.n_gx, z.n_gy, z.n_gz
     gx, gy, gz = (lax.axis_index(a) for a in ("gx", "gy", "gz"))
@@ -307,7 +345,10 @@
 
     barrier = pltpu.get_barrier_semaphore()
     for r in range(1, n_gz):
-        pl.semaphore_signal(barrier, inc=1, device_id=along_z(r), device_id_type=mesh_type)
+
+        @pl.when(r > gz)
+        def _(r=r):
+            pl.semaphore_signal(barrier, inc=1, device_id=along_z(r), device_id_type=mesh_type)
 
     def greet(dx, carry):
         pl.semaphore_signal(barrier, inc=1, device_id=along_x(dx), device_id_type=mesh_type)
@@ -326,34 +367,49 @@
     ]
     for c in loads:
         c.start()
-    for c in loads[:-1]:
-        c.wait()
-    params_of(z, cells, offs, e_index, r_index, exponents, pm)
-    cols[0, 0, :TOP] = coefficients(z, basis, blocks)
-    cols[0, 0, TOP:] = pm[...]
-
-    def body(ytab, ztab, t, zs, d, zd):
+    with jax.named_scope("load_wait"):
+        for c in loads[:-1]:
+            c.wait()
+    with jax.named_scope("coefs"):
+        params_of(z, cells, offs, e_index, r_index, exponents, pm)
+        cols[0, 0, :TOP] = coefficients(z, basis, blocks)
+        cols[0, 0, TOP:] = pm[...]
+
+    def body(ytab, ztab, t0, t1, t2, t3, zs, d, zw, yw, te):
         s = Scratch()
-        s.t, s.z, s.d, s.zd, s.h, s.hd, s.ea, s.acc, s.dacc = t, zs, d, zd, h, hd, ea, acc, dacc
-        kyc = iota_f((z.nky, 1), 0) + (gx * z.nky).astype(f32)
-        kzc = jnp.concatenate(
-            [iota_f((z.nkz, 1), 0) + kz_start(z, gy, gz, dy) for dy in range(n_gy)], axis=0
-        )
-        ytab[...] = span_table(kyc, z.ny)
-        ztab[...] = span_table(kzc, z.nz)
-        for ref in (acc, dacc):
-            ref[...] = jnp.zeros_like(ref)
-        pl.semaphore_wait(barrier, n_gz + n_gx + n_gy - 3)
-
-        def copy_z(r):
+        s.ytab, s.ztab, s.t, s.z = ytab, ztab, (t0, t1, t2, t3), zs
+        s.d, s.zw, s.yw, s.te = d, zw, yw, te
+        s.h, s.hd, s.fy, s.fe = h, hd, fy, fe
+        s.acc, s.dacc, s.eacc = acc, dacc, eacc
+        with jax.named_scope("clear"):
+            for ref in (acc, dacc, eacc):
+                ref[...] = jnp.zeros_like(ref)
+        with jax.named_scope("barrier_wait"):
+            pl.semaphore_wait(barrier, n_gx + n_gy - 2 + gz)
+
+        def copy_z(q):
+            target = along_z(q)
+            slot = jnp.where(target[2] < n_gz // 2, q, n_gz - q)
             return pltpu.make_async_remote_copy(
                 src_ref=cols.at[0, 0],
-                dst_ref=cols.at[r, 0],
-                send_sem=send_z.at[r],
-                recv_sem=recv_z.at[r],
-                device_id=along_z(r),
+                dst_ref=cols.at[slot, 0],
+                send_sem=send_z.at[q],
+                recv_sem=recv_z.at[slot],
+                device_id=target,
                 device_id_type=mesh_type,
             )
+
+        def wait_z(r):
+            with jax.named_scope(f"z_wait{r}"):
+                pltpu.make_async_remote_copy(
+                    src_ref=cols.at[0, 0],
+                    dst_ref=cols.at[r, 0],
+                    send_sem=send_z.at[r],
+                    recv_sem=recv_z.at[r],
+                    device_id=along_z(r),
+                    device_id_type=mesh_type,
+                ).wait_recv()
+            forward(r)
 
         def copy_c(r, dx):
             return pltpu.make_async_remote_copy(
@@ -373,32 +429,66 @@
             lax.fori_loop(1, n_gx, one, 0)
 
         for r in range(1, n_gz):
-            copy_z(r).start()
+
+            @pl.when(r <= gz)
+            def _(r=r):
+                pl.semaphore_signal(
+                    ready.at[n_gz - r], inc=1, device_id=along_z(r), device_id_type=mesh_type
+                )
+                copy_z(r).start()
+
         forward(0)
-        for r in range(1, n_gz - 1):
-            copy_z(r).wait_recv()
-            forward(r)
-
-        def step(c, carry):
+        with jax.named_scope("tables"):
+            y_table(z, place, ytab)
+            z_tables(z, place, ztab)
+        def send_up(distance):
+            @pl.when(gz + distance < n_gz)
+            def _():
+                pl.semaphore_wait(ready.at[n_gz - distance], 1)
+                copy_z(n_gz - distance).start()
+
+        send_up(1)
+        wait_z(1)
+        for distance in range(2, n_gz - 1):
+            send_up(distance)
+
+        def arrive(r, g):
+            with jax.named_scope("x_wait"):
+                for d in range(z.per):
+                    dx = g * z.per + d
+
+                    @pl.when(dx > 0)
+                    def _(dx=dx):
+                        copy_c(r, dx).wait_recv()
+
+            unpack(z, [cols[r, g * z.per + d] for d in range(z.per)], prm)
+
+        lower = gz < n_gz // 2
+
+        def second():
+            send_up(n_gz - 1)
+            for r in range(2, n_gz - 1):
+                wait_z(r)
+
+            @pl.when(lower)
+            def _():
+                wait_z(n_gz - 1)
+
+        def third():
+            @pl.when(jnp.logical_not(lower))
+            def _():
+                wait_z(n_gz - 1)
+
+        def chunk(c, carry):
             r, g = c // z.groups, c % z.groups
-
-            @pl.when(c == z.groups)
-            def _():
-                copy_z(n_gz - 1).wait_recv()
-                forward(n_gz - 1)
-
-            for d in range(z.per):
-                dx = g * z.per + d
-
-                @pl.when(dx > 0)
-                def _(dx=dx):
-                    copy_c(r, dx).wait_recv()
-
-            unpack(z, [cols[r, g * z.per + d] for d in range(z.per)], prm)
-            chunk_work(z, place, prm, ytab, ztab, s)
+            pl.when(c == z.groups)(second)
+            pl.when(c == 2 * z.groups)(third)
+            arrive(r, g)
+            with jax.named_scope("chunk"):
+                chunk_work(z, place, r, prm, s)
             return carry
 
-        lax.fori_loop(0, n_gz * z.groups, step, 0)
+        lax.fori_loop(0, n_gz * z.groups - 1, chunk, 0)
 
         def copy_d(which):
             return pltpu.make_async_remote_copy(
@@ -422,26 +512,37 @@
             )
 
         loads[-1].wait()
+
+        def x_transform(g):
+            v = acc[2 * z.wide * g : 2 * z.wide * (g + 1)]
+            hi, lo = split(v)
+            for kk in range(z.kys):
+                parts = [
+                    w[m * z.wide + kk * z.nx : m * z.wide + (kk + 1) * z.nx]
+                    for w in (hi, lo, hi)
+                    for m in range(2)
+                ]
+                q = jnp.dot(xt[...], jnp.concatenate(parts, axis=0), preferred_element_type=f32)
+                out = q[: z.nx] + swapped(z, q[z.nx :])
+                start = g * z.wide + kk * z.nx
+                rows = slice(start, start + z.nx)
+                own[rows] = out[:, : 2 * z.nkz]
+                for dy in range(1, n_gy):
+                    give[dy - 1, rows] = out[:, 2 * z.nkz * dy : 2 * z.nkz * (dy + 1)]
+
+        arrive(n_gz - 1, z.groups - 1)
+        with jax.named_scope("last"):
+            chunk_work(z, place, n_gz - 1, prm, s, x_transform)
+        for which in range(2):
+            copy_d(which).start()
         for g in range(z.blocks):
-            hi, lo = split(acc[2 * z.wide * g : 2 * z.wide * (g + 1)])
-            q = jnp.dot(
-                xt[...], jnp.concatenate([hi, lo, hi], axis=0), preferred_element_type=f32
-            )
-            out = q[: z.wide] + swapped(z, q[z.wide :])
-            rows = slice(g * z.wide, (g + 1) * z.wide)
-            own[rows] = out[:, : 2 * z.nkz]
+            x_transform(g)
+        for g in range(z.blocks):
             for dy in range(1, n_gy):
-                give[dy - 1, rows] = out[:, 2 * z.nkz * dy : 2 * z.nkz * (dy + 1)]
-            if g == 0:
-                for which in range(2):
-                    copy_d(which).start()
-            else:
-                for dy in range(1, n_gy):
-                    copy_e(dy, g - 1).start()
-        for dy in range(1, n_gy):
-            copy_e(dy, z.blocks - 1).start()
-        for r in range(1, n_gz):
-            copy_z(r).wait_send()
+                copy_e(dy, g).start()
+        with jax.named_scope("drain"):
+            for r in range(1, n_gz):
+                copy_z(r).wait_send()
 
         def drain(c, carry):
             @pl.when(c % n_gx > 0)
@@ -451,21 +552,35 @@
             return carry
 
         lax.fori_loop(0, n_gz * n_gx, drain, 0)
-        for which in range(2):
-            copy_d(which).wait()
-        for g in range(z.blocks):
-            for dy in range(1, n_gy):
-                copy_e(dy, g).wait()
+        with jax.named_scope("exchange_wait"):
+            for which in range(2):
+                copy_d(which).wait()
+            for g in range(z.blocks):
+                for dy in range(1, n_gy):
+                    copy_e(dy, g).wait()
 
     pl.run_scoped(
         body,
-        pltpu.VMEM((2 * z.nky, 3 * SPAN), bf16),
-        pltpu.VMEM((z.cols, 3 * SPAN), bf16),
-        pltpu.VMEM((2, 2 * z.wide, 3 * DEPTH), bf16),
+        pltpu.VMEM((2 * z.nky, 3 * CYW), bf16),
+        pltpu.VMEM((n_gz, z.cols, 3 * CZW), bf16),
+        *[pltpu.VMEM((2 * z.wide, 3 * DEPTH), bf16)] * TS,
         pltpu.VMEM((z.cols, 3 * DEPTH), bf16),
         pltpu.VMEM((CX * CYW, 3 * DEPTH), bf16),
-        pltpu.VMEM((CZ, 3 * DEPTH), bf16),
+        pltpu.VMEM((3 * CZW, DEPTH), bf16),
+        pltpu.VMEM((3 * CYW, DEPTH), bf16),
+        pltpu.VMEM((CX * HALO, 3 * DEPTH), bf16),
     )
+
+
+def add_edges(dacc, eacc):
+    lane = lax.broadcasted_iota(jnp.int32, (CYW, LANES), 1)
+    pad = jnp.zeros((CYW, LANES - CX * HALO), f32)
+    for which, start in ((0, LANES - HALO), (1, 0)):
+        e = jnp.concatenate([eacc[which], pad], axis=1)
+        mask = (lane >= start) & (lane < start + HALO)
+        for x in range(CX):
+            v = pltpu.roll(e, (start - x * HALO) % LANES, 1)
+            dacc[x] = dacc[x] + jnp.where(mask, v, 0.0)
 
 
 def finish(z, own, got, dacc, edges, dens_ref, spec_ref):
@@ -482,8 +597,7 @@
 def x_table(z):
     idx = np.arange(z.nx)
     angle = (idx[:, None] * idx[None, :] % z.nx) * (2.0 * math.pi / z.nx)
-    eye = np.eye(z.kys)
-    c, s = np.kron(eye, np.cos(angle)), np.kron(eye, np.sin(angle))
+    c, s = np.cos(angle), np.sin(angle)
     full = np.block([[c, s], [s, -c]]) / math.sqrt(z.nx * z.ny * z.nz)
     full = full.astype(np.float32)
     hi = full.astype(ml_dtypes.bfloat16)
@@ -528,10 +642,13 @@
             pltpu.VMEM((COEFS + 8, LANES), f32),
             pltpu.VMEM((n_gz, n_gx, BLOCK_ROWS, LANES), f32),
             pltpu.VMEM((n_gy - 1, z.rows, 2 * z.nkz), f32),
-            pltpu.VMEM((SIDE * SIDE, 2 * z.nky, LANES), f32),
+            pltpu.VMEM((SIDE * SIDE, z.blocks, 2 * z.kys, LANES), f32),
             pltpu.VMEM((SIDE * SIDE, CX, LANES), f32),
-            pltpu.VMEM((2, n_gy * z.nkz // 8, LANES), f32),
+            pltpu.VMEM((SIDE, CYW, LANES), f32),
+            pltpu.VMEM((2, SIDE, HALO, LANES), f32),
             pltpu.VMEM((2 * z.rows, z.cols), f32),
+            pltpu.VMEM((2, CYW, CX * HALO), f32),
+            pltpu.SemaphoreType.REGULAR((n_gz,)),
             dma((8,)),
             dma((n_gz,)),
             dma((n_gz,)),

time: 22.8 us -> 21 us (0.921)
  the two profiles are of different devices: /device:TPU:0 before, /device:TPU:17 now
where the time goes in v3:
time: 21 us; the launch traced here: 20.9 us
  Pallas kernels  20.2 us (96%)
  between operations  0.64 us (3%)
    pallas_call x1, Pallas kernels, shards(): pl.pallas_call(functools.partial(kernel, z), out_shape=[jax.ShapeDtypeStr...  19.3 us
    pallas_call x1, Pallas kernels, shards(): pl.pallas_call(functools.partial(finish, z), out_shape=[jax.ShapeDtypeStr...  0.93 us

profile of v3, /device:TPU:17, one launch (start us, length us, event | category | flops | bytes accessed | tf_op | source)
XLA Modules:
  0.0 20.9 jit_solution(15911238292039322450)
XLA Ops:
  0.6 19.3 %shard_map.95 = (f32[512,128]{1,0:T(8,128)S(1)}, f32[1,512,128]{2,1,0:T(8,128)S(1)}, f32[8,48,128]{2,1,0:T(8,128)S(1)}, f32[2,8,8,128]{3,2,1,0:T(8,128)S(1)}) custom-call(f32[64,529]{1,0:T(8,128)} %bitcast.7, f32[32,529]{1,0:T(8,128)} %bitcast.8, s32[3,32]{1,0:T(4,128)} %cells_hbm.1, f32[3,32]{1,0:T(4,128)} %offs_hbm.1, s32[1,32]{1,0:T(1,128)} %bitcast.9, ...), custom_call_target="tpu_custom_call" | custom-call | tf_op jit(solution)/shard_map/pallas_call | solution.py:622
  19.9 0.9 %shard_map.96 = (f32[8,32,128]{2,1,0:T(8,128)}, f32[2,512,64]{2,1,0:T(8,128)}) custom-call(f32[512,128]{1,0:T(8,128)S(1)} %get-tuple-element.8.own, f32[1,512,128]{2,1,0:T(8,128)S(1)} %get-tuple-element.9.got, f32[8,48,128]{2,1,0:T(8,128)S(1)} %get-tuple-element.10.dacc, f32[2,8,8,128]{3,2,1,0:T(8,128)S(1)} %get-tuple-element.11.edges), custom_call_target="tpu_custom_call" | custom-call | tf_op jit(solution)/shard_map/pallas_call | solution.py:671

commit v4 on v3

--- a/solution.py
+++ b/solution.py
@@ -198,6 +198,36 @@
         hi, lo = split(v)
         put3(s.z, slice(0, z.cols), k, hi, lo, (0, 0, 1))
 
+    def build(g):
+        for m in range(2):
+            for kk in range(z.kys):
+                o = m * z.wide + kk * nx
+                for k in range(SIDE):
+                    v = None
+                    for i in range(SIDE):
+                        q = m * z.kys + kk
+                        w = s.h[k * SIDE + i, g, q : q + 1, :] * fx[i]
+                        v = w if v is None else v + w
+                    hi, lo = split(v)
+                    put3(s.t[g % TS], slice(o, o + nx), k, hi, lo, (0, 1, 0))
+
+    def product(g):
+        rows = slice(2 * z.wide * g, 2 * z.wide * (g + 1))
+        s.acc[rows] = s.acc[rows] + nt(s.t[g % TS][...], s.z[...])
+
+    if after is not None:
+        density_work(z, place, r, s)
+        add_edges(s.dacc, s.eacc)
+    build(0)
+    for g in range(1, z.blocks):
+        build(g)
+        product(g - 1)
+    product(z.blocks - 1)
+
+
+def density_work(z, place, r, s):
+    near = jnp.where(place[2] < z.n_gz // 2, 0, 1)
+
     def cells():
         for x in range(CX):
             for k in range(SIDE):
@@ -227,33 +257,8 @@
         more = nt(jnp.concatenate([hi, lo, hi], axis=1), s.te[...])
         s.eacc[which] = s.eacc[which] + more
 
-    def build(g):
-        for m in range(2):
-            for kk in range(z.kys):
-                o = m * z.wide + kk * nx
-                for k in range(SIDE):
-                    v = None
-                    for i in range(SIDE):
-                        q = m * z.kys + kk
-                        w = s.h[k * SIDE + i, g, q : q + 1, :] * fx[i]
-                        v = w if v is None else v + w
-                    hi, lo = split(v)
-                    put3(s.t[g % TS], slice(o, o + nx), k, hi, lo, (0, 1, 0))
-
-    def product(g):
-        rows = slice(2 * z.wide * g, 2 * z.wide * (g + 1))
-        s.acc[rows] = s.acc[rows] + nt(s.t[g % TS][...], s.z[...])
-
-    near = jnp.where(gz < z.n_gz // 2, 0, 1)
-    if after is not None:
+    if isinstance(r, int):
         edge(1 - near)
-        add_edges(s.dacc, s.eacc)
-    build(0)
-    for g in range(1, z.blocks):
-        build(g)
-        product(g - 1)
-    product(z.blocks - 1)
-    if after is not None:
         return
     pl.when(r == 0)(cells)
     pl.when(r == 1)(lambda: edge(near))
@@ -327,7 +332,7 @@
     own, got, dacc, edges,
     basis, blocks, cells, offs, e_index, r_index, exponents, xt, pm, prm, cols, give,
     h, hd, fy, fe, acc, eacc,
-    ready, in_sem, send_z, recv_z, send_c, recv_c, send_e, recv_e, send_d, recv_d,
+    ready, in_sem, recv_z, recv_c, recv_e, recv_d,
 ):
     n_gx, n_gy, n_gz = z.n_gx, z.n_gy, z.n_gz
     gx, gy, gz = (lax.axis_index(a) for a in ("gx", "gy", "gz"))
@@ -381,11 +386,10 @@
         s.d, s.zw, s.yw, s.te = d, zw, yw, te
         s.h, s.hd, s.fy, s.fe = h, hd, fy, fe
         s.acc, s.dacc, s.eacc = acc, dacc, eacc
-        with jax.named_scope("clear"):
-            for ref in (acc, dacc, eacc):
-                ref[...] = jnp.zeros_like(ref)
         with jax.named_scope("barrier_wait"):
             pl.semaphore_wait(barrier, n_gx + n_gy - 2 + gz)
+
+        send_z, send_c, send_e, send_d = (in_sem.at[n] for n in range(4))
 
         def copy_z(q):
             target = along_z(q)
@@ -393,8 +397,8 @@
             return pltpu.make_async_remote_copy(
                 src_ref=cols.at[0, 0],
                 dst_ref=cols.at[slot, 0],
-                send_sem=send_z.at[q],
-                recv_sem=recv_z.at[slot],
+                send_sem=send_z,
+                recv_sem=recv_z.at[slot - 1],
                 device_id=target,
                 device_id_type=mesh_type,
             )
@@ -404,8 +408,8 @@
                 pltpu.make_async_remote_copy(
                     src_ref=cols.at[0, 0],
                     dst_ref=cols.at[r, 0],
-                    send_sem=send_z.at[r],
-                    recv_sem=recv_z.at[r],
+                    send_sem=send_z,
+                    recv_sem=recv_z.at[r - 1],
                     device_id=along_z(r),
                     device_id_type=mesh_type,
                 ).wait_recv()
@@ -415,8 +419,8 @@
             return pltpu.make_async_remote_copy(
                 src_ref=cols.at[r, 0],
                 dst_ref=cols.at[r, dx],
-                send_sem=send_c.at[r * n_gx + dx],
-                recv_sem=recv_c.at[r * n_gx + dx],
+                send_sem=send_c,
+                recv_sem=recv_c.at[r * z.groups + dx // z.per],
                 device_id=along_x(dx),
                 device_id_type=mesh_type,
             )
@@ -433,40 +437,47 @@
             @pl.when(r <= gz)
             def _(r=r):
                 pl.semaphore_signal(
-                    ready.at[n_gz - r], inc=1, device_id=along_z(r), device_id_type=mesh_type
+                    ready.at[n_gz - r - 1], inc=1, device_id=along_z(r), device_id_type=mesh_type
                 )
                 copy_z(r).start()
 
         forward(0)
         with jax.named_scope("tables"):
+            for ref in (acc, dacc, eacc):
+                ref[...] = jnp.zeros_like(ref)
             y_table(z, place, ytab)
             z_tables(z, place, ztab)
         def send_up(distance):
             @pl.when(gz + distance < n_gz)
             def _():
-                pl.semaphore_wait(ready.at[n_gz - distance], 1)
+                pl.semaphore_wait(ready.at[n_gz - distance - 1], 1)
                 copy_z(n_gz - distance).start()
 
         send_up(1)
         wait_z(1)
-        for distance in range(2, n_gz - 1):
+        for distance in range(2, n_gz):
             send_up(distance)
 
         def arrive(r, g):
+            def blocks_in(ref):
+                pltpu.make_async_copy(ref, ref, recv_c.at[r * z.groups + g]).wait()
+
             with jax.named_scope("x_wait"):
-                for d in range(z.per):
-                    dx = g * z.per + d
-
-                    @pl.when(dx > 0)
-                    def _(dx=dx):
-                        copy_c(r, dx).wait_recv()
+                first = lambda: blocks_in(cols.at[r, pl.ds(1, z.per - 1)])
+                if z.groups == 1:
+                    first()
+                else:
+                    pl.when(g == 0)(first)
+
+                    @pl.when(g > 0)
+                    def _():
+                        blocks_in(cols.at[r, pl.ds(g * z.per, z.per)])
 
             unpack(z, [cols[r, g * z.per + d] for d in range(z.per)], prm)
 
         lower = gz < n_gz // 2
 
         def second():
-            send_up(n_gz - 1)
             for r in range(2, n_gz - 1):
                 wait_z(r)
 
@@ -481,11 +492,13 @@
 
         def chunk(c, carry):
             r, g = c // z.groups, c % z.groups
-            pl.when(c == z.groups)(second)
-            pl.when(c == 2 * z.groups)(third)
             arrive(r, g)
+            pl.when(c == z.groups)(third)
             with jax.named_scope("chunk"):
                 chunk_work(z, place, r, prm, s)
+            pl.when(c == z.groups - 1)(second)
+            with jax.named_scope("dens"):
+                density_work(z, place, r, s)
             return carry
 
         lax.fori_loop(0, n_gz * z.groups - 1, chunk, 0)
@@ -494,19 +507,21 @@
             return pltpu.make_async_remote_copy(
                 src_ref=dacc.at[:, pl.ds(which * (CY + HALO), HALO), :],
                 dst_ref=edges.at[which],
-                send_sem=send_d.at[which],
-                recv_sem=recv_d.at[which],
+                send_sem=send_d,
+                recv_sem=recv_d.at[0],
                 device_id=along_y(2 * which - 1),
                 device_id_type=mesh_type,
             )
 
-        def copy_e(dy, g):
-            rows = pl.ds(g * z.wide, z.wide)
+        half = z.rows // 2
+
+        def copy_e(dy, part):
+            rows = pl.ds(part * half, half)
             return pltpu.make_async_remote_copy(
                 src_ref=give.at[dy - 1, rows],
                 dst_ref=got.at[dy - 1, rows],
-                send_sem=send_e.at[dy * z.blocks + g],
-                recv_sem=recv_e.at[dy * z.blocks + g],
+                send_sem=send_e,
+                recv_sem=recv_e.at[dy - 1],
                 device_id=along_y(dy),
                 device_id_type=mesh_type,
             )
@@ -535,29 +550,24 @@
             chunk_work(z, place, n_gz - 1, prm, s, x_transform)
         for which in range(2):
             copy_d(which).start()
-        for g in range(z.blocks):
-            x_transform(g)
-        for g in range(z.blocks):
+        for part in range(2):
+            for g in range(z.blocks // 2):
+                x_transform(part * z.blocks // 2 + g)
             for dy in range(1, n_gy):
-                copy_e(dy, g).start()
+                copy_e(dy, part).start()
+
+        def done(ref, sem):
+            pltpu.make_async_copy(ref, ref, sem).wait()
+
         with jax.named_scope("drain"):
-            for r in range(1, n_gz):
-                copy_z(r).wait_send()
-
-        def drain(c, carry):
-            @pl.when(c % n_gx > 0)
-            def _():
-                copy_c(c // n_gx, c % n_gx).wait_send()
-
-            return carry
-
-        lax.fori_loop(0, n_gz * n_gx, drain, 0)
+            done(cols.at[0, pl.ds(0, n_gz - 1)], send_z)
+            done(cols.at[:, pl.ds(1, n_gx - 1)], send_c)
         with jax.named_scope("exchange_wait"):
-            for which in range(2):
-                copy_d(which).wait()
-            for g in range(z.blocks):
-                for dy in range(1, n_gy):
-                    copy_e(dy, g).wait()
+            done(edges, send_d)
+            done(edges, recv_d.at[0])
+            done(give, send_e)
+            for dy in range(1, n_gy):
+                done(got.at[dy - 1], recv_e.at[dy - 1])
 
     pl.run_scoped(
         body,
@@ -611,7 +621,8 @@
     n_gx, n_gy, n_gz = (lax.axis_size(a) for a in ("gx", "gy", "gz"))
     pair_dev = pair_blocks.shape[1]
     z = Sizes(n_gx, n_gy, n_gz, pair_dev)
-    assert FOLD * pair_dev == LANES and n_gx % z.per == 0 and n_gz >= 3 and n_gy >= 2
+    assert FOLD * pair_dev == LANES and n_gx % z.per == 0 and n_gz >= 3 and n_gy >= 2 and z.blocks % 2 == 0
+    assert n_gx >= n_gz
     in_vmem = pl.BlockSpec(memory_space=pltpu.VMEM)
     in_hbm = pl.BlockSpec(memory_space=pltpu.HBM)
     basis = basis_map.T
@@ -648,16 +659,12 @@
             pltpu.VMEM((2, SIDE, HALO, LANES), f32),
             pltpu.VMEM((2 * z.rows, z.cols), f32),
             pltpu.VMEM((2, CYW, CX * HALO), f32),
-            pltpu.SemaphoreType.REGULAR((n_gz,)),
+            pltpu.SemaphoreType.REGULAR((n_gz - 1,)),
             dma((8,)),
-            dma((n_gz,)),
-            dma((n_gz,)),
-            dma((n_gz * n_gx,)),
-            dma((n_gz * n_gx,)),
-            dma((n_gy * z.blocks,)),
-            dma((n_gy * z.blocks,)),
-            dma((2,)),
-            dma((2,)),
+            dma((n_gz - 1,)),
+            dma((n_gz * z.groups,)),
+            dma((n_gy - 1,)),
+            dma((1,)),
         ],
         compiler_params=pltpu.CompilerParams(
             collective_id=0, has_side_effects=True, vmem_limit_bytes=VMEM_LIMIT

time: 21 us -> 19.5 us (0.929)
  the two profiles are of different devices: /device:TPU:17 before, /device:TPU:0 now
where the time goes in v4:
time: 19.5 us; the launch traced here: 19.3 us
  Pallas kernels  18.7 us (96%)
  between operations  0.64 us (3%)
    pallas_call x1, Pallas kernels, shards(): pl.pallas_call(functools.partial(kernel, z), out_shape=[jax.ShapeDtypeStr...  17.8 us
    pallas_call x1, Pallas kernels, shards(): pl.pallas_call(functools.partial(finish, z), out_shape=[jax.ShapeDtypeStr...  0.93 us

profile of v4, /device:TPU:0, one launch (start us, length us, event | category | flops | bytes accessed | tf_op | source)
XLA Modules:
  0.0 19.3 jit_solution(12508125189765012205)
XLA Ops:
  0.6 17.8 %shard_map.95 = (f32[512,128]{1,0:T(8,128)S(1)}, f32[1,512,128]{2,1,0:T(8,128)S(1)}, f32[8,48,128]{2,1,0:T(8,128)S(1)}, f32[2,8,8,128]{3,2,1,0:T(8,128)S(1)}) custom-call(f32[64,529]{1,0:T(8,128)} %bitcast.7, f32[32,529]{1,0:T(8,128)} %bitcast.8, s32[3,32]{1,0:T(4,128)} %cells_hbm.1, f32[3,32]{1,0:T(4,128)} %offs_hbm.1, s32[1,32]{1,0:T(1,128)} %bitcast.9, ...), custom_call_target="tpu_custom_call" | custom-call | tf_op jit(solution)/shard_map/pallas_call | solution.py:633
  18.4 0.9 %shard_map.96 = (f32[8,32,128]{2,1,0:T(8,128)}, f32[2,512,64]{2,1,0:T(8,128)}) custom-call(f32[512,128]{1,0:T(8,128)S(1)} %get-tuple-element.8.own, f32[1,512,128]{2,1,0:T(8,128)S(1)} %get-tuple-element.9.got, f32[8,48,128]{2,1,0:T(8,128)S(1)} %get-tuple-element.10.dacc, f32[2,8,8,128]{3,2,1,0:T(8,128)S(1)} %get-tuple-element.11.edges), custom_call_target="tpu_custom_call" | custom-call | tf_op jit(solution)/shard_map/pallas_call | solution.py:678

commit v5 on v4

--- a/solution.py
+++ b/solution.py
@@ -192,11 +192,12 @@
         s.fe[0, k] = fz[k][CZ + HALO :]
         s.fe[1, k] = fz[k][CZ : CZ + HALO]
         stack3(s.zw, k, fz[k])
-    for k in range(SIDE):
-        lanes = slice(k * LANES, (k + 1) * LANES)
-        v = jnp.dot(s.ztab[r], s.zw[:, lanes], preferred_element_type=f32)
-        hi, lo = split(v)
-        put3(s.z, slice(0, z.cols), k, hi, lo, (0, 0, 1))
+    for k in range(0, SIDE, 2):
+        two = s.zw[:, k * LANES : (k + 2) * LANES]
+        v = jnp.dot(s.ztab[r], two, preferred_element_type=f32)
+        for n in range(2):
+            hi, lo = split(v[:, n * LANES : (n + 1) * LANES])
+            put3(s.z, slice(0, z.cols), k + n, hi, lo, (0, 0, 1))
 
     def build(g):
         for m in range(2):
@@ -287,14 +288,9 @@
 def coefficients(z, basis, blocks):
     bh, bl = split(basis[...])
     ph, pb = split(blocks[...])
-    ph = jnp.concatenate([ph] * FOLD, axis=0)
-    pb = jnp.concatenate([pb] * FOLD, axis=0)
-    both = nt(bh, ph) + (nt(bh, pb) + nt(bl, ph))
-    lane = lax.broadcasted_iota(jnp.int32, (TOP, FOLD * z.pair_dev), 1) // z.pair_dev
-    v = both[:TOP]
-    for g in range(1, FOLD):
-        v = jnp.where(lane == g, both[g * TOP : (g + 1) * TOP], v)
-    return v
+    both = nt(jnp.concatenate([bh, bl], axis=0), ph)
+    v = both[:COEFS] + (both[COEFS:] + nt(bh, pb))
+    return jnp.concatenate([v[g * TOP : (g + 1) * TOP] for g in range(FOLD)], axis=1)
 
 
 def unpack(z, blocks, prm):

time: 19.5 us -> 19.3 us (0.990)
  Pallas kernels: 18.7 us -> 18.5 us
    pallas_call x1, Pallas kernels: 17.8 us -> 17.5 us  [shards(): pl.pallas_call(functools.partial(kernel, z), out_shape=[jax.ShapeDtypeStr...]
where the time goes in v5:
time: 19.3 us; the launch traced here: 19.1 us
  Pallas kernels  18.5 us (96%)
  between operations  0.64 us (3%)
    pallas_call x1, Pallas kernels, shards(): pl.pallas_call(functools.partial(kernel, z), out_shape=[jax.ShapeDtypeStr...  17.5 us
    pallas_call x1, Pallas kernels, shards(): pl.pallas_call(functools.partial(finish, z), out_shape=[jax.ShapeDtypeStr...  0.93 us

profile of v5, /device:TPU:0, one launch (start us, length us, event | category | flops | bytes accessed | tf_op | source)
XLA Modules:
  0.0 19.1 jit_solution(9780268182180376221)
XLA Ops:
  0.6 17.5 %shard_map.95 = (f32[512,128]{1,0:T(8,128)S(1)}, f32[1,512,128]{2,1,0:T(8,128)S(1)}, f32[8,48,128]{2,1,0:T(8,128)S(1)}, f32[2,8,8,128]{3,2,1,0:T(8,128)S(1)}) custom-call(f32[64,529]{1,0:T(8,128)} %bitcast.7, f32[32,529]{1,0:T(8,128)} %bitcast.8, s32[3,32]{1,0:T(4,128)} %cells_hbm.1, f32[3,32]{1,0:T(4,128)} %offs_hbm.1, s32[1,32]{1,0:T(1,128)} %bitcast.9, ...), custom_call_target="tpu_custom_call" | custom-call | tf_op jit(solution)/shard_map/pallas_call | solution.py:629
  18.2 0.9 %shard_map.96 = (f32[8,32,128]{2,1,0:T(8,128)}, f32[2,512,64]{2,1,0:T(8,128)}) custom-call(f32[512,128]{1,0:T(8,128)S(1)} %get-tuple-element.8.own, f32[1,512,128]{2,1,0:T(8,128)S(1)} %get-tuple-element.9.got, f32[8,48,128]{2,1,0:T(8,128)S(1)} %get-tuple-element.10.dacc, f32[2,8,8,128]{3,2,1,0:T(8,128)S(1)} %get-tuple-element.11.edges), custom_call_target="tpu_custom_call" | custom-call | tf_op jit(solution)/shard_map/pallas_call | solution.py:674

commit v6 on v5

--- a/solution.py
+++ b/solution.py
@@ -219,6 +219,8 @@
     if after is not None:
         density_work(z, place, r, s)
         add_edges(s.dacc, s.eacc)
+    else:
+        density_work(z, place, r, s, 1)
     build(0)
     for g in range(1, z.blocks):
         build(g)
@@ -226,7 +228,7 @@
     product(z.blocks - 1)
 
 
-def density_work(z, place, r, s):
+def density_work(z, place, r, s, part=0):
     near = jnp.where(place[2] < z.n_gz // 2, 0, 1)
 
     def cells():
@@ -242,7 +244,7 @@
         more = nt(s.d[...], jnp.concatenate([hi, hi, lo], axis=1))
         s.dacc[...] = s.dacc[...] + more.reshape(CX, CYW, CZ)
 
-    def edge(which):
+    def edge(which, on=True):
         for x in range(0, CX, 2):
             for j in range(SIDE):
                 both = []
@@ -256,15 +258,16 @@
                 put3(s.te, slice(x * HALO, (x + 2) * HALO), j, hi, lo, (0, 0, 1))
         hi, lo = s.yw[:CYW], s.yw[CYW : 2 * CYW]
         more = nt(jnp.concatenate([hi, lo, hi], axis=1), s.te[...])
-        s.eacc[which] = s.eacc[which] + more
+        s.eacc[which] = s.eacc[which] + jnp.where(on, more, 0.0)
 
     if isinstance(r, int):
         edge(1 - near)
         return
-    pl.when(r == 0)(cells)
-    pl.when(r == 1)(lambda: edge(near))
-    if z.groups > 1:
-        pl.when(r == z.n_gz - 1)(lambda: edge(1 - near))
+    if part == 0:
+        pl.when(r == 0)(cells)
+        return
+    far = r == z.n_gz - 1
+    edge(jnp.where(far, 1 - near, near), (r == 1) | far)
 
 
 class Scratch:

time: 19.3 us -> 19.2 us (level)
  no operation moved by 1% of the time
where the time goes in v6:
time: 19.2 us; the launch traced here: 19.1 us
  Pallas kernels  18.5 us (96%)
  between operations  0.64 us (3%)
    pallas_call x1, Pallas kernels, shards(): pl.pallas_call(functools.partial(kernel, z), out_shape=[jax.ShapeDtypeStr...  17.5 us
    pallas_call x1, Pallas kernels, shards(): pl.pallas_call(functools.partial(finish, z), out_shape=[jax.ShapeDtypeStr...  0.93 us

profile of v6, /device:TPU:0, one launch (start us, length us, event | category | flops | bytes accessed | tf_op | source)
XLA Modules:
  0.0 19.1 jit_solution(5273179483717973294)
XLA Ops:
  0.6 17.5 %shard_map.95 = (f32[512,128]{1,0:T(8,128)S(1)}, f32[1,512,128]{2,1,0:T(8,128)S(1)}, f32[8,48,128]{2,1,0:T(8,128)S(1)}, f32[2,8,8,128]{3,2,1,0:T(8,128)S(1)}) custom-call(f32[64,529]{1,0:T(8,128)} %bitcast.7, f32[32,529]{1,0:T(8,128)} %bitcast.8, s32[3,32]{1,0:T(4,128)} %cells_hbm.1, f32[3,32]{1,0:T(4,128)} %offs_hbm.1, s32[1,32]{1,0:T(1,128)} %bitcast.9, ...), custom_call_target="tpu_custom_call" | custom-call | tf_op jit(solution)/shard_map/pallas_call | solution.py:632
  18.2 0.9 %shard_map.96 = (f32[8,32,128]{2,1,0:T(8,128)}, f32[2,512,64]{2,1,0:T(8,128)}) custom-call(f32[512,128]{1,0:T(8,128)S(1)} %get-tuple-element.8.own, f32[1,512,128]{2,1,0:T(8,128)S(1)} %get-tuple-element.9.got, f32[8,48,128]{2,1,0:T(8,128)S(1)} %get-tuple-element.10.dacc, f32[2,8,8,128]{3,2,1,0:T(8,128)S(1)} %get-tuple-element.11.edges), custom_call_target="tpu_custom_call" | custom-call | tf_op jit(solution)/shard_map/pallas_call | solution.py:677
